TPU v7x, 32 devices: a whole 2x2x4 slice. The times are simulated.
32 devices in a mesh: band: 4 (over x, core), pw: 8 (over z, y).
Axes of the slice: x: 2, y: 2, z: 4, core: 2. Of those that a mesh axis runs over, the one named last changes fastest.
Arguments:
- wave_coeffs: float32 [32768, 512], P('pw', 'band'), may hold values from -6 to 6
- miller: int32 [3, 32768], P(None, 'pw'), may hold values from -32 to 31, as said below
- atom_types: int32 [32], replicated, may hold values from 0 to 3
- positions: float32 [3, 32], replicated, may hold values from 0 to 1
- sphere_radii: float32 [4], replicated, may hold values from 3.5 to 5
- h_blocks: float32 [4, 64, 64], replicated, may hold values from -3 to 3
- potential: float32 [64, 64, 64], P('pw'), may hold values from -2 to 2
Outputs:
- h_applied: float32 [32768, 512], P('pw', 'band')
- subspace: float32 [512, 512], P('pw', 'band')
Inputs may be any that keep to these rules, and one draw needn't show every extreme that they name: `miller`: the plane waves are distinct grid points after wrapping mod 64. The plane waves of the k-th of 8 equal contiguous blocks have wrapped z index in k * 8 to (k + 1) * 8 - 1.
All inputs are finite; a program needn't handle non-finite values.
Results may differ from a plain program's by a relative error of at most 0.0003.
Values sent between devices are 32-bit elements; how exact they have to be, the bound alone decides.
No kernel may reach another device: no remote copies, remote signals or barrier semaphores. Data moves between devices by JAX's collectives and lax.ppermute only.
A program may use at most 128 MiB of HBM per device.

v0:
```python
import math

import jax
import jax.numpy as jnp
import numpy as np
from jax import lax
from jax.sharding import PartitionSpec as P

NPW = 32768


PRECISE = lax.Precision.HIGHEST


def double_factorial(value):
    result = 1
    while value > 1:
        result = result * value
        value = value - 2
    return float(result)


def bessel_table(argument, count):
    safe = jnp.maximum(argument, 1.0)
    upward = [jnp.sin(safe) / safe, jnp.sin(safe) / (safe * safe) - jnp.cos(safe) / safe]
    for degree in range(1, count - 1):
        upward.append((2 * degree + 1) / safe * upward[degree] - upward[degree - 1])
    half_square = -0.5 * argument * argument
    power = jnp.ones_like(argument)
    columns = []
    for degree in range(count):
        term = jnp.ones_like(argument)
        total = jnp.ones_like(argument)
        for index in range(1, 17):
            term = term * half_square / float(index * (2 * degree + 2 * index + 1))
            total = total + term
        series = power * total / double_factorial(2 * degree + 1)
        power = power * argument
        columns.append(jnp.where(argument > degree + 1, upward[degree], series))
    return jnp.stack(columns, axis=-1)


def harmonic_table(unit, count):
    along_x, along_y, along_z = (unit[0], unit[1], unit[2])
    ones = jnp.ones_like(along_z)
    cosines = [ones]
    sines = [jnp.zeros_like(along_z)]
    for azimuth in range(1, count):
        cosines.append(along_x * cosines[-1] - along_y * sines[-1])
        sines.append(along_x * sines[-2 + 1] + along_y * cosines[-2])
    legendre = {}
    for azimuth in range(count):
        legendre[azimuth, azimuth] = double_factorial(2 * azimuth - 1) * ones
        if azimuth + 1 < count:
            legendre[azimuth + 1, azimuth] = (
                (2 * azimuth + 1) * along_z * legendre[azimuth, azimuth]
            )
        for degree in range(azimuth + 2, count):
            legendre[degree, azimuth] = (
                (2 * degree - 1) * along_z * legendre[degree - 1, azimuth]
                - (degree + azimuth - 1) * legendre[degree - 2, azimuth]
            ) / float(degree - azimuth)
    columns = []
    for degree in range(count):
        for signed in range(-degree, degree + 1):
            azimuth = abs(signed)
            weight = math.sqrt(
                (2 * degree + 1)
                * math.factorial(degree - azimuth)
                / (4.0 * math.pi * math.factorial(degree + azimuth))
            )
            if azimuth > 0:
                weight = weight * math.sqrt(2.0)
            circle = cosines[azimuth] if signed >= 0 else sines[azimuth]
            columns.append(weight * legendre[degree, azimuth] * circle)
    return jnp.stack(columns, axis=-1)


def cas_matrix(grid_size):
    across = jnp.arange(grid_size, dtype=jnp.int32)
    phase = across[:, None] * across[None, :] % grid_size
    angle = 2.0 * math.pi / grid_size * phase.astype(jnp.float32)
    return (jnp.cos(angle) + jnp.sin(angle)) / math.sqrt(grid_size)


def transform_across(table, field):
    field = jnp.einsum("ai,zijb->zajb", table, field, precision=PRECISE)
    return jnp.einsum("aj,zijb->ziab", table, field, precision=PRECISE)


def matching_block(
    miller_float,
    radial_all,
    angular,
    positions,
    type_onehot,
    degree_onehot,
    first,
    width,
    tile_scale,
):
    funcs_each = angular.shape[1]
    row_ids = first + jnp.arange(width, dtype=jnp.int32)
    atom_ids = row_ids // funcs_each
    pick_atom = (
        atom_ids[:, None] == jnp.arange(positions.shape[1], dtype=jnp.int32)[None, :]
    ).astype(jnp.float32)
    pick_func = (
        (row_ids % funcs_each)[:, None] == jnp.arange(funcs_each, dtype=jnp.int32)[None, :]
    ).astype(jnp.float32)
    centres = jnp.dot(positions, pick_atom.T, precision=PRECISE)
    row_types = jnp.dot(pick_atom, type_onehot, precision=PRECISE)
    row_degrees = jnp.dot(pick_func, degree_onehot, precision=PRECISE)
    pick_radial = (row_types[:, :, None] * row_degrees[:, None, :]).reshape(
        width, radial_all.shape[1]
    )
    radial = jnp.dot(radial_all, pick_radial.T, precision=PRECISE)
    harmonic = jnp.dot(angular, pick_func.T, precision=PRECISE)
    angle = 2.0 * math.pi * jnp.dot(miller_float.T, centres, precision=PRECISE)
    return (jnp.cos(angle) + jnp.sin(angle)) * radial * harmonic * tile_scale


def per_device(wave_coeffs, miller, atom_types, positions, sphere_radii, h_blocks, potential):
    pw_count = lax.axis_size("pw")
    pw_index = lax.axis_index("pw")
    local_waves, local_bands = wave_coeffs.shape
    grid_size = potential.shape[1]
    funcs_each = h_blocks.shape[1]
    type_count = h_blocks.shape[0]
    degree_count = math.isqrt(funcs_each)
    atom_total = atom_types.shape[0]
    factor = NPW ** (-0.5)
    tile_scale = 4.0 * math.pi * NPW ** (-0.5)
    miller_float = miller.astype(jnp.float32)
    squares = jnp.sum(miller_float * miller_float, axis=0)
    miller_norm = jnp.sqrt(squares)
    kinetic = squares / 1536.0
    wrapped = jnp.mod(miller, grid_size)
    table = cas_matrix(grid_size)
    type_onehot = (atom_types[:, None] == jnp.arange(type_count, dtype=jnp.int32)[None, :]).astype(
        jnp.float32
    )
    degree_of = np.repeat(np.arange(degree_count), 2 * np.arange(degree_count) + 1)
    degree_onehot = (
        jnp.asarray(degree_of, dtype=jnp.int32)[:, None]
        == jnp.arange(degree_count, dtype=jnp.int32)[None, :]
    ).astype(jnp.float32)
    unit = miller_float / jnp.maximum(miller_norm, 1.0)
    angular = harmonic_table(unit, degree_count)
    argument = sphere_radii[None, :] * miller_norm[:, None] * (2.0 / grid_size)
    radial_all = bessel_table(argument, degree_count).reshape(
        local_waves, type_count * degree_count
    )

    def tile_at(first, width):
        return matching_block(
            miller_float,
            radial_all,
            angular,
            positions,
            type_onehot,
            degree_onehot,
            first,
            width,
            tile_scale,
        )

    empty = jnp.zeros((local_waves, local_bands), jnp.float32)
    count = atom_total * funcs_each
    width = math.gcd(count, 512)

    def one_block(turn):
        return jnp.einsum(
            "gk,gb->kb", tile_at(0 + turn * width, width), wave_coeffs, precision=PRECISE
        )

    spheres = lax.psum(
        lax.map(one_block, jnp.arange(count // width, dtype=jnp.int32)).reshape(count, local_bands),
        "pw",
    )
    count = type_onehot.shape[0]
    chosen = jnp.einsum("at,tfk->afk", type_onehot, h_blocks, precision=PRECISE)
    shaped = spheres.reshape(count, funcs_each, local_bands)
    piece = jnp.einsum("afk,akb->afb", chosen, shaped, precision=PRECISE).reshape(
        count * funcs_each, local_bands
    )
    count = piece.shape[0]
    add_width = math.gcd(count, 512)

    def add_block(turn, running):
        first = turn * add_width
        values = lax.dynamic_slice_in_dim(piece, first, add_width, 0)
        return running + jnp.dot(tile_at(0 + first, add_width), values, precision=PRECISE)

    muffin = lax.fori_loop(0, count // add_width, add_block, empty)
    planes_each = grid_size // pw_count
    flat_index = (
        (wrapped[2] - pw_index * planes_each) * grid_size * grid_size
        + wrapped[0] * grid_size
        + wrapped[1]
    )
    slab_grid = (
        jnp.zeros((planes_each * grid_size * grid_size, local_bands), jnp.float32)
        .at[flat_index]
        .set(wave_coeffs)
    )
    slab_grid = transform_across(
        table, slab_grid.reshape(planes_each, grid_size, grid_size, local_bands)
    )
    turned = jnp.transpose(potential, (2, 0, 1))
    field = jnp.einsum(
        "cz,zxyb->cxyb",
        table,
        lax.all_to_all(slab_grid, "pw", split_axis=1, concat_axis=0, tiled=True),
        precision=PRECISE,
    )
    weighted = field * turned[..., None]
    back_field = jnp.einsum("cz,zxyb->cxyb", table, weighted, precision=PRECISE)
    slab_grid = lax.all_to_all(back_field, "pw", split_axis=0, concat_axis=1, tiled=True)
    slab_grid = transform_across(table, slab_grid)
    inter = slab_grid.reshape(planes_each * grid_size * grid_size, local_bands)[flat_index]
    h_applied = kinetic[:, None] * wave_coeffs + inter + muffin
    columns = lax.all_gather(wave_coeffs, "band", axis=1, tiled=True)
    subspace = lax.psum_scatter(
        jnp.einsum("gi,gj->ij", columns, h_applied, precision=PRECISE) * factor,
        "pw",
        scatter_dimension=0,
        tiled=True,
    )
    return (h_applied, subspace)


def solution(mesh):
    in_specs = (P("pw", "band"), P(None, "pw"), P(), P(), P(), P(), P("pw", None, None))
    out_specs = (P("pw", "band"), P("pw", "band"))
    return jax.shard_map(
        per_device, mesh=mesh, in_specs=in_specs, out_specs=out_specs, check_vma=False
    )
```

profile of v0, /device:TPU:0, one launch (start us, length us, event | category | flops | bytes accessed | tf_op | source)
XLA Modules:
  0.0 1494.1 jit_solution(10544018742020567742)
XLA Ops:
  9.1 17.7 %scatter_custom_fusion = f32[32768,128]{1,0:T(8,128)} fusion(s32[4096]{0:T(1024)S(1)} %bitcast.293, f32[4096,128]{1,0:T(8,128)} %param.12, f32[]{:T(128)} %constant.612.clone.1), kind=kCustom, calls=%fused_computation.113 | custom fusion | bytes 16777728 | tf_op jit(solution)/shard_map/scatter | solution.py:205
  26.8 33.4 %fusion.95 = f32[8,64,64,128]{3,1,2,0:T(8,128)} fusion(f32[8,64,64,128]{3,2,1,0:T(8,128)} %bitcast.285), kind=kOutput, calls=%fused_computation.109 | convolution fusion | flops 3221291008 | bytes 33554432 | tf_op jit(solution)/shard_map/ai,zijb->zajb/dot_general | solution.py:87
  60.2 33.9 %fusion.98 = f32[8,64,64,128]{3,2,1,0:T(8,128)} fusion(f32[8,64,64,128]{3,1,2,0:T(8,128)} %fusion.95), kind=kOutput, calls=%fused_computation.110 | convolution fusion | flops 3221291008 | bytes 33554432 | tf_op jit(solution)/shard_map/aj,zijb->ziab/dot_general | solution.py:88
  94.1 11.8 copy.55
  105.9 7.4 all-to-all-start
  122.3 354.0 %all-to-all-done = f32[8,64,64,128]{3,2,0,1:T(8,128)} async-done(((f32[8,64,64,128]{3,2,0,1:T(8,128)}), f32[8,64,64,128]{3,2,0,1:T(8,128)}, u32[]{:S(2)}, u32[]{:S(2)}) %all-to-all-start) | async-done | bytes 16777248 | tf_op jit(solution)/shard_map/all_to_all | solution.py:214
  476.4 11.8 copy.57
  488.2 33.4 %fusion.87 = f32[64,8,64,128]{3,0,2,1:T(8,128)} fusion(f32[64,8,64,128]{3,2,1,0:T(8,128)} %bitcast.288), kind=kOutput, calls=%fused_computation.101 | convolution fusion | flops 3221291008 | bytes 33554432 | tf_op jit(solution)/shard_map/cz,zxyb->cxyb/dot_general | solution.py:211
  521.6 20.8 %fusion.93 = f32[64,8,64,128]{3,0,2,1:T(8,128)S(1)} fusion(f32[64,8,64,128]{3,0,2,1:T(8,128)} %fusion.87, f32[64,8,64]{0,2,1:T(8,128)S(1)} %bitcast.292), kind=kOutput, calls=%fused_computation.107 | convolution fusion | flops 3225485312 | bytes 33685504 | tf_op jit(solution)/shard_map/cz,zxyb->cxyb/dot_general | solution.py:218
  542.5 19.3 %copy.59 = f32[64,8,64,128]{3,2,1,0:T(8,128)} copy(f32[64,8,64,128]{3,0,2,1:T(8,128)S(1)} %fusion.93) | data formatting | bytes 33554432 | tf_op jit(solution)/shard_map/cz,zxyb->cxyb/dot_general | solution.py:218
  561.8 5.8 all-to-all-start.1
  573.2 359.2 %while.29 = (s32[]{:T(128)}, f32[4,512,128]{2,1,0:T(8,128)}, s32[4]{0:T(128)S(1)}, f32[3,32]{1,0:T(4,128)S(1)}, f32[3,4096]{1,0:T(4,128)S(1)}, /*index=5*/f32[40...) while((s32[]{:T(128)}, f32[4,512,128]{2,1,0:T(8,128)}, ...), condition=%wide.region_3.4_spmd.clone, body=%wide.region_2.3_spmd.clone.sunk | while | flops 5727775744 | bytes 62776748 | solution.py:178
  575.3 8.5 fusion.438
  584.2 6.8 fusion.440
  594.5 68.5 %fusion.441 = f32[4,512,128]{2,1,0:T(8,128)} fusion(f32[4,512,128]{2,1,0:T(8,128)} %get-tuple-element.825, s32[]{:T(128)} %get-tuple-element.824, f32[4096,128]{1,0:T(8,128)S(1)} %copy-done.3, f32[512,4096]{1,0:T(8,128)S(1)} %fusion.435, f32[512,4096]{1,0:T(8,128)S(1)} %fusion.438, f32[512,4096]{1,0:T(8,128)S(1)} %fusion.440), kind=kOutput, calls=%fused_computation.17.clone.2 | convolution fusion | flops 3231711232 | bytes 27525632 | tf_op jit(solution)/shard_map/while/body/eval_jaxpr/gk,gb->kb/dot_general | solution.py:173
  665.0 8.5 fusion.438
  673.8 6.8 fusion.440
  684.2 68.5 %fusion.441 = f32[4,512,128]{2,1,0:T(8,128)} fusion(f32[4,512,128]{2,1,0:T(8,128)} %get-tuple-element.825, s32[]{:T(128)} %get-tuple-element.824, f32[4096,128]{1,0:T(8,128)S(1)} %copy-done.3, f32[512,4096]{1,0:T(8,128)S(1)} %fusion.435, f32[512,4096]{1,0:T(8,128)S(1)} %fusion.438, f32[512,4096]{1,0:T(8,128)S(1)} %fusion.440), kind=kOutput, calls=%fused_computation.17.clone.2 | convolution fusion | flops 3231711232 | bytes 27525632 | tf_op jit(solution)/shard_map/while/body/eval_jaxpr/gk,gb->kb/dot_general | solution.py:173
  754.6 8.5 fusion.438
  763.5 6.8 fusion.440
  773.8 68.5 %fusion.441 = f32[4,512,128]{2,1,0:T(8,128)} fusion(f32[4,512,128]{2,1,0:T(8,128)} %get-tuple-element.825, s32[]{:T(128)} %get-tuple-element.824, f32[4096,128]{1,0:T(8,128)S(1)} %copy-done.3, f32[512,4096]{1,0:T(8,128)S(1)} %fusion.435, f32[512,4096]{1,0:T(8,128)S(1)} %fusion.438, f32[512,4096]{1,0:T(8,128)S(1)} %fusion.440), kind=kOutput, calls=%fused_computation.17.clone.2 | convolution fusion | flops 3231711232 | bytes 27525632 | tf_op jit(solution)/shard_map/while/body/eval_jaxpr/gk,gb->kb/dot_general | solution.py:173
  844.3 8.5 fusion.438
  853.1 6.8 fusion.440
  863.5 68.5 %fusion.441 = f32[4,512,128]{2,1,0:T(8,128)} fusion(f32[4,512,128]{2,1,0:T(8,128)} %get-tuple-element.825, s32[]{:T(128)} %get-tuple-element.824, f32[4096,128]{1,0:T(8,128)S(1)} %copy-done.3, f32[512,4096]{1,0:T(8,128)S(1)} %fusion.435, f32[512,4096]{1,0:T(8,128)S(1)} %fusion.438, f32[512,4096]{1,0:T(8,128)S(1)} %fusion.440), kind=kOutput, calls=%fused_computation.17.clone.2 | convolution fusion | flops 3231711232 | bytes 27525632 | tf_op jit(solution)/shard_map/while/body/eval_jaxpr/gk,gb->kb/dot_general | solution.py:173
  935.3 76.9 %all-reduce.2.cloned.1.call-done = f32[32,64,128]{2,1,0:T(8,128)} async-done(((f32[32,64,128]{2,1,0:T(8,128)}), f32[32,64,128]{2,1,0:T(8,128)}) %all-reduce.2.cloned.1.call-update) | async-done | bytes 1048592 | tf_op jit(solution)/shard_map/psum | solution.py:177
  1015.4 295.7 %while.30 = (s32[]{:T(128)}, f32[4096,128]{1,0:T(8,128)}, f32[3,32]{1,0:T(4,128)S(1)}, f32[3,4096]{1,0:T(4,128)S(1)}, f32[4096,32]{1,0:T(8,128)}, /*index=5*/f32...) while((s32[]{:T(128)}, f32[4096,128]{1,0:T(8,128)}, ...), condition=%wide.region_6.7_spmd.clone, body=%wide.region_5.6_spmd.clone.sunk | while | flops 5728824320 | bytes 56484792 | solution.py:195
  1016.1 10.2 fusion.455
  1026.6 9.0 fusion.457
  1035.6 5.7 fusion.452
  1041.3 48.0 %fusion.458 = f32[4096,128]{1,0:T(8,128)} fusion(f32[512,4096]{1,0:T(8,128)} %fusion.452, f32[512,4096]{1,0:T(8,128)} %fusion.455, f32[512,4096]{1,0:T(8,128)} %fusion.457, f32[4096,128]{1,0:T(8,128)} %get-tuple-element.862, pred[]{:T(512)S(6)} %compare.33, f32[2048,128]{1,0:T(8,128)S(1)} %get-tuple-element.880, s32[]{:T(128)S(6)} %select_n.255), kind=kOutput, calls=%fused_computation.59.clone.3 | convolution fusion | flops 3232759808 | bytes 29622276 | tf_op jit(solution)/shard_map/while/body/eval_jaxpr/dot_general | solution.py:193
  1090.0 10.2 fusion.455
  1100.5 9.0 fusion.457
  1109.5 5.7 fusion.452
  1115.2 48.0 %fusion.458 = f32[4096,128]{1,0:T(8,128)} fusion(f32[512,4096]{1,0:T(8,128)} %fusion.452, f32[512,4096]{1,0:T(8,128)} %fusion.455, f32[512,4096]{1,0:T(8,128)} %fusion.457, f32[4096,128]{1,0:T(8,128)} %get-tuple-element.862, pred[]{:T(512)S(6)} %compare.33, f32[2048,128]{1,0:T(8,128)S(1)} %get-tuple-element.880, s32[]{:T(128)S(6)} %select_n.255), kind=kOutput, calls=%fused_computation.59.clone.3 | convolution fusion | flops 3232759808 | bytes 29622276 | tf_op jit(solution)/shard_map/while/body/eval_jaxpr/dot_general | solution.py:193
  1163.9 10.2 fusion.455
  1174.4 9.0 fusion.457
  1183.4 5.7 fusion.452
  1189.1 48.0 %fusion.458 = f32[4096,128]{1,0:T(8,128)} fusion(f32[512,4096]{1,0:T(8,128)} %fusion.452, f32[512,4096]{1,0:T(8,128)} %fusion.455, f32[512,4096]{1,0:T(8,128)} %fusion.457, f32[4096,128]{1,0:T(8,128)} %get-tuple-element.862, pred[]{:T(512)S(6)} %compare.33, f32[2048,128]{1,0:T(8,128)S(1)} %get-tuple-element.880, s32[]{:T(128)S(6)} %select_n.255), kind=kOutput, calls=%fused_computation.59.clone.3 | convolution fusion | flops 3232759808 | bytes 29622276 | tf_op jit(solution)/shard_map/while/body/eval_jaxpr/dot_general | solution.py:193
  1237.8 10.2 fusion.455
  1248.3 9.0 fusion.457
  1257.3 5.7 fusion.452
  1263.1 48.0 %fusion.458 = f32[4096,128]{1,0:T(8,128)} fusion(f32[512,4096]{1,0:T(8,128)} %fusion.452, f32[512,4096]{1,0:T(8,128)} %fusion.455, f32[512,4096]{1,0:T(8,128)} %fusion.457, f32[4096,128]{1,0:T(8,128)} %get-tuple-element.862, pred[]{:T(512)S(6)} %compare.33, f32[2048,128]{1,0:T(8,128)S(1)} %get-tuple-element.880, s32[]{:T(128)S(6)} %select_n.255), kind=kOutput, calls=%fused_computation.59.clone.3 | convolution fusion | flops 3232759808 | bytes 29622276 | tf_op jit(solution)/shard_map/while/body/eval_jaxpr/dot_general | solution.py:193
  1311.0 11.8 copy.60
  1322.9 33.4 %fusion.101 = f32[8,64,64,128]{3,1,2,0:T(8,128)} fusion(f32[8,64,64,128]{3,2,1,0:T(8,128)} %bitcast.286), kind=kOutput, calls=%fused_computation.111 | convolution fusion | flops 3221291008 | bytes 33554432 | tf_op jit(solution)/shard_map/ai,zijb->zajb/dot_general | solution.py:87
  1356.3 33.7 %fusion.83 = f32[8,64,128,64]{2,3,1,0:T(8,128)} fusion(f32[8,64,64,128]{3,1,2,0:T(8,128)} %fusion.101), kind=kOutput, calls=%fused_computation.97 | convolution fusion | flops 3221291008 | bytes 33554432 | tf_op jit(solution)/shard_map/aj,zijb->ziab/dot_general | solution.py:88
  1390.0 20.1 %gather_fusion = f32[4096,128]{1,0:T(8,128)} fusion(f32[32768,128]{1,0:T(8,128)} %bitcast.287, s32[4096]{0:T(1024)S(1)} %copy-done.10), kind=kCustom, calls=%fused_computation | custom fusion | bytes 4210688 | tf_op jit(solution)/shard_map/gather | solution.py:221
  1413.7 10.0 fusion.107
  1424.5 61.8 %reduce-scatter.4.cloned.1.call-done = f32[64,128]{1,0:T(8,128)} async-done(((f32[512,128]{1,0:T(8,128)}), f32[64,128]{1,0:T(8,128)}) %reduce-scatter.4.cloned.1.call-update) | async-done | bytes 32784
  (117 shorter events, 50.7 us)
Async XLA Ops:
  8.0 925.7 %copy-start = (f32[4,64,64]{2,1,0:T(8,128)S(1)}, f32[4,64,64]{2,1,0:T(8,128)}, u32[]{:S(2)}) copy-start(f32[4,64,64]{2,1,0:T(8,128)} %param.17) | copy-start | bytes 196612
  9.1 17.7 %copy-start.8 = (s32[4096,1]{0,1:T(1,128)}, s32[4096,1]{0,1:T(1,128)S(1)}, u32[]{:S(2)}) copy-start(s32[4096,1]{0,1:T(1,128)S(1)} %compare_select_fusion) | copy-start | bytes 49156
  105.9 7.4 copy-start.5
  105.9 8.9 copy-start.11
  105.9 370.5 %all-to-all-start = ((f32[8,64,64,128]{3,2,0,1:T(8,128)}), f32[8,64,64,128]{3,2,0,1:T(8,128)}, u32[]{:S(2)}, u32[]{:S(2)}) async-start(f32[8,64,64,128]{3,2,0,1:T(8,128)} %copy.55), calls=%async_computation | async-start | bytes 33554432 | tf_op jit(solution)/shard_map/all_to_all | solution.py:214
  121.6 366.6 %copy-start.4 = (f32[4096,4,8]{0,1,2:T(4,128)}, f32[4096,4,8]{0,1,2:T(4,128)S(1)}, u32[]{:S(2)}) copy-start(f32[4096,4,8]{0,1,2:T(4,128)S(1)} %fusion.152) | copy-start | bytes 1572868
  488.2 33.5 %copy-start.6 = (f32[8,64,64]{2,1,0:T(8,128)S(1)}, f32[8,64,64]{2,1,0:T(8,128)}, u32[]{:S(2)}) copy-start(f32[8,64,64]{2,1,0:T(8,128)} %param.18) | copy-start | bytes 393220
  561.8 749.3 %all-to-all-start.1 = ((f32[64,8,64,128]{3,2,1,0:T(8,128)}), f32[64,8,64,128]{3,2,1,0:T(8,128)}, u32[]{:S(2)}, u32[]{:S(2)}) async-start(f32[64,8,64,128]{3,2,1,0:T(8,128)} %copy.59), calls=%async_computation.1 | async-start | bytes 33554432 | tf_op jit(solution)/shard_map/all_to_all | solution.py:219
  567.5 5.7 copy-start.12
  567.6 5.6 copy-start.13
  567.6 5.6 copy-start.14
  567.6 444.5 %all-reduce.2.cloned.1.call-start = ((), (), s32[]{:S(2)}) async-start(), calls=%async_computation.3 | async-start | bytes 2097152 | tf_op jit(solution)/shard_map/psum | solution.py:177
  573.2 359.8 %copy-start.9 = (s32[4096,1]{0,1:T(1,128)S(1)}, s32[4096,1]{0,1:T(1,128)}, u32[]{:S(2)}) copy-start(s32[4096,1]{0,1:T(1,128)} %copy-done.8) | copy-start | bytes 49156
  590.9 3.6 copy-start.3
  680.6 3.6 copy-start.3
  770.2 3.6 copy-start.3
  859.9 3.6 copy-start.3
  932.4 481.3 %all-gather.2.cloned.1.call-start = ((), (), s32[]{:S(2)}) async-start(), calls=%async_computation.4 | async-start | bytes 10485760 | tf_op jit(solution)/shard_map/all_gather | solution.py:223
  933.0 553.4 %reduce-scatter.4.cloned.1.call-start = ((), (), s32[]{:S(2)}) async-start(), calls=%async_computation.5 | async-start | bytes 294912
  1356.3 33.7 %copy-start.10 = (s32[4096]{0:T(1024)S(1)}, s32[4096]{0:T(1024)}, u32[]{:S(2)}) copy-start(s32[4096]{0:T(1024)} %broadcast_clamp_fusion) | copy-start | bytes 49156
  1390.0 20.1 %copy-start.2 = (f32[4096,128]{1,0:T(8,128)S(1)}, f32[4096,128]{1,0:T(8,128)}, u32[]{:S(2)}) copy-start(f32[4096,128]{1,0:T(8,128)} %get-tuple-element.354) | copy-start | bytes 6291460
  1390.0 20.1 %copy-start.7 = (f32[4096]{0:T(1024)S(1)}, f32[4096]{0:T(1024)}, u32[]{:S(2)}) copy-start(f32[4096]{0:T(1024)} %get-tuple-element.655) | copy-start | bytes 49156
  1410.2 76.2 %copy-start.1 = (f32[4,64,64]{2,1,0:T(8,128)S(1)}, f32[4,64,64]{2,1,0:T(8,128)}, u32[]{:S(2)}) copy-start(f32[4,64,64]{2,1,0:T(8,128)} %param.17) | copy-start | bytes 196612
Sparse Core Ops, SparseCore 0:
  932.5 79.5 all-reduce.1
  1424.6 61.6 reduce-scatter.3
Sparse Core Ops, SparseCore 1:
  934.4 60.5 all-gather.1
where the time goes:
time: 1500 us; the launch traced here: 1490 us
  matrix products  852 us (57%)
  waiting for transfers between devices  493 us (33%)
  local copies, waits for them, and re-layouts  101 us (7%)
  between operations  16.1 us (1%)
    all_to_all x1, waiting for transfers between devices, per_device(): lax.all_to_all(slab_grid, 'pw', split_axis=1, concat_axis=0, tiled=True)  354 us
    dot_general x4, matrix products, one_block(): jnp.einsum('gk,gb->kb', tile_at(0 + turn * width, width), wave_coeffs, pr...  274 us
    dot_general x4, matrix products, add_block(): jnp.dot(tile_at(0 + first, add_width), values, precision=PRECISE)  192 us
    psum x1, waiting for transfers between devices, per_device(): lax.psum(lax.map(one_block, jnp.arange(count // width, dtype=jnp.int32))....  76.9 us
    dot_general x8, matrix products, matching_block(): radial = jnp.dot(radial_all, pick_radial.T, precision=PRECISE)  75 us
    dot_general x2, matrix products, transform_across(): return jnp.einsum('aj,zijb->ziab', table, field, precision=PRECISE)  67.6 us
    dot_general x2, matrix products, transform_across(): field = jnp.einsum('ai,zijb->zajb', table, field, precision=PRECISE)  66.8 us
    dot_general x8, matrix products, matching_block(): angle = 2.0 * math.pi * jnp.dot(miller_float.T, centres, precision=PRECISE)  63 us
  transfers between devices with their start and end apart: 5, of which 3 were waited for; matrix products, arithmetic and copies ran while one was open for 52% of the time, Pallas kernels for 0%

commit v1 on v0

v1 whole, which is shorter than its diff:
```python
import functools
import math

import jax
import jax.numpy as jnp
import numpy as np
from jax import lax
from jax.experimental import pallas as pl
from jax.experimental.pallas import tpu as pltpu
from jax.sharding import PartitionSpec as P

NPW = 32768


PRECISE = lax.Precision.HIGHEST


def double_factorial(value):
    result = 1
    while value > 1:
        result = result * value
        value = value - 2
    return float(result)


def bessel_table(argument, count):
    safe = jnp.maximum(argument, 1.0)
    upward = [jnp.sin(safe) / safe, jnp.sin(safe) / (safe * safe) - jnp.cos(safe) / safe]
    for degree in range(1, count - 1):
        upward.append((2 * degree + 1) / safe * upward[degree] - upward[degree - 1])
    half_square = -0.5 * argument * argument
    power = jnp.ones_like(argument)
    columns = []
    for degree in range(count):
        term = jnp.ones_like(argument)
        total = jnp.ones_like(argument)
        for index in range(1, 17):
            term = term * half_square / float(index * (2 * degree + 2 * index + 1))
            total = total + term
        series = power * total / double_factorial(2 * degree + 1)
        power = power * argument
        columns.append(jnp.where(argument > degree + 1, upward[degree], series))
    return columns


def harmonic_table(unit, count):
    along_x, along_y, along_z = (unit[0], unit[1], unit[2])
    ones = jnp.ones_like(along_z)
    cosines = [ones]
    sines = [jnp.zeros_like(along_z)]
    for azimuth in range(1, count):
        cosines.append(along_x * cosines[-1] - along_y * sines[-1])
        sines.append(along_x * sines[-2 + 1] + along_y * cosines[-2])
    legendre = {}
    for azimuth in range(count):
        legendre[azimuth, azimuth] = double_factorial(2 * azimuth - 1) * ones
        if azimuth + 1 < count:
            legendre[azimuth + 1, azimuth] = (
                (2 * azimuth + 1) * along_z * legendre[azimuth, azimuth]
            )
        for degree in range(azimuth + 2, count):
            legendre[degree, azimuth] = (
                (2 * degree - 1) * along_z * legendre[degree - 1, azimuth]
                - (degree + azimuth - 1) * legendre[degree - 2, azimuth]
            ) / float(degree - azimuth)
    columns = []
    for degree in range(count):
        for signed in range(-degree, degree + 1):
            azimuth = abs(signed)
            weight = math.sqrt(
                (2 * degree + 1)
                * math.factorial(degree - azimuth)
                / (4.0 * math.pi * math.factorial(degree + azimuth))
            )
            if azimuth > 0:
                weight = weight * math.sqrt(2.0)
            circle = cosines[azimuth] if signed >= 0 else sines[azimuth]
            columns.append(weight * legendre[degree, azimuth] * circle)
    return columns


def cas_matrix(grid_size):
    across = jnp.arange(grid_size, dtype=jnp.int32)
    phase = across[:, None] * across[None, :] % grid_size
    angle = 2.0 * math.pi / grid_size * phase.astype(jnp.float32)
    return (jnp.cos(angle) + jnp.sin(angle)) / math.sqrt(grid_size)


def split_bf16(value):
    high = value.astype(jnp.bfloat16)
    low = (value - high.astype(jnp.float32)).astype(jnp.bfloat16)
    return high, low


def dot32(left, right):
    return jnp.dot(left, right, preferred_element_type=jnp.float32)


def params(*semantics):
    return pltpu.CompilerParams(
        dimension_semantics=semantics or None, vmem_limit_bytes=56 * 1024 * 1024
    )


def fill_matching(types_ref, table_ref, phase_ref, high_ref, low_ref):
    atoms = phase_ref.shape[0]
    funcs = table_ref.shape[1]

    def one(atom, carry):
        tile = table_ref[types_ref[atom]] * phase_ref[pl.ds(atom, 1), :]
        high, low = split_bf16(tile)
        start = pl.multiple_of(atom * funcs, funcs)
        high_ref[pl.ds(start, funcs), :] = high
        low_ref[pl.ds(start, funcs), :] = low
        return carry

    lax.fori_loop(0, atoms, one, 0, unroll=4)


def fill_tables(miller_ref, places_ref, radii_ref, table_ref, phase_ref, angular_ref, spacing):
    kinds, funcs, _ = table_ref.shape
    degree_count = math.isqrt(funcs)
    miller = miller_ref[...].astype(jnp.float32)
    along = [miller[axis : axis + 1, :] for axis in range(3)]
    norm = jnp.sqrt(along[0] * along[0] + along[1] * along[1] + along[2] * along[2])
    scale = jnp.maximum(norm, 1.0)
    for index, column in enumerate(harmonic_table([part / scale for part in along], degree_count)):
        angular_ref[index : index + 1, :] = column
    argument = radii_ref[...] * norm * spacing
    weight = 4.0 * math.pi * NPW ** (-0.5)
    for degree, column in enumerate(bessel_table(argument, degree_count)):
        first, last = degree * degree, (degree + 1) * (degree + 1)
        rows = angular_ref[first:last, :]
        for kind in range(kinds):
            table_ref[kind, first:last, :] = rows * (column[kind : kind + 1, :] * weight)
    places = places_ref[...]
    turns = sum(places[:, axis : axis + 1] * along[axis] for axis in range(3))
    angle = 2.0 * math.pi * (turns - jnp.round(turns))
    phase_ref[...] = jnp.cos(angle) + jnp.sin(angle)


def sphere_kernel(
    types_ref,
    miller_ref,
    places_ref,
    radii_ref,
    wave_ref,
    out_ref,
    table_ref,
    phase_ref,
    angular_ref,
    high_ref,
    low_ref,
    *,
    spacing,
):
    bands = wave_ref.shape[1]

    @pl.when(pl.program_id(0) == 0)
    def _():
        out_ref[...] = jnp.zeros_like(out_ref)

    fill_tables(miller_ref, places_ref, radii_ref, table_ref, phase_ref, angular_ref, spacing)
    fill_matching(types_ref, table_ref, phase_ref, high_ref, low_ref)
    wave_high, wave_low = split_bf16(wave_ref[...])
    both = jnp.concatenate([wave_high, wave_low], axis=1)
    rows = out_ref.shape[0]
    step = math.gcd(rows, 512)
    for first in range(0, rows, step):
        main = dot32(high_ref[first : first + step, :], both)
        rest = dot32(low_ref[first : first + step, :], wave_high)
        out_ref[first : first + step, :] += main[:, :bands] + main[:, bands:] + rest


def sphere_call(types, miller, positions, radii, wave, kinds, funcs, spacing):
    waves, bands = wave.shape
    atoms = positions.shape[1]
    block = math.gcd(waves, 512)
    rows = atoms * funcs
    return pl.pallas_call(
        functools.partial(sphere_kernel, spacing=spacing),
        grid=(waves // block,),
        in_specs=[
            pl.BlockSpec(memory_space=pltpu.SMEM),
            pl.BlockSpec((3, block), lambda i: (0, i)),
            pl.BlockSpec((atoms, 3), lambda i: (0, 0)),
            pl.BlockSpec((kinds, 1), lambda i: (0, 0)),
            pl.BlockSpec((block, bands), lambda i: (i, 0)),
        ],
        out_specs=[
            pl.BlockSpec((rows, bands), lambda i: (0, 0)),
            pl.BlockSpec((kinds, funcs, block), lambda i: (0, 0, i)),
            pl.BlockSpec((atoms, block), lambda i: (0, i)),
        ],
        out_shape=[
            jax.ShapeDtypeStruct((rows, bands), jnp.float32),
            jax.ShapeDtypeStruct((kinds, funcs, waves), jnp.float32),
            jax.ShapeDtypeStruct((atoms, waves), jnp.float32),
        ],
        scratch_shapes=[
            pltpu.VMEM((funcs, block), jnp.float32),
            pltpu.VMEM((rows, block), jnp.bfloat16),
            pltpu.VMEM((rows, block), jnp.bfloat16),
        ],
        compiler_params=params("arbitrary"),
        cost_estimate=pl.CostEstimate(
            flops=6 * waves * rows * bands, bytes_accessed=8 * waves * bands, transcendentals=0
        ),
        name="sphere",
    )(types, miller, positions.T, radii[:, None], wave)


def muffin_kernel(types_ref, table_ref, phase_ref, sphere_ref, out_ref, high_ref, low_ref):
    bands = out_ref.shape[0]
    fill_matching(types_ref, table_ref, phase_ref, high_ref, low_ref)
    high, low = split_bf16(sphere_ref[...])
    main = dot32(jnp.concatenate([high, low], axis=0), high_ref[...])
    rest = dot32(high, low_ref[...])
    out_ref[...] = main[:bands, :] + main[bands:, :] + rest


def muffin_call(types, table, phase, sphere):
    kinds, funcs, waves = table.shape
    atoms = phase.shape[0]
    bands, rows = sphere.shape
    block = math.gcd(waves, 512)
    return pl.pallas_call(
        muffin_kernel,
        grid=(waves // block,),
        in_specs=[
            pl.BlockSpec(memory_space=pltpu.SMEM),
            pl.BlockSpec((kinds, funcs, block), lambda i: (0, 0, i)),
            pl.BlockSpec((atoms, block), lambda i: (0, i)),
            pl.BlockSpec((bands, rows), lambda i: (0, 0)),
        ],
        out_specs=pl.BlockSpec((bands, block), lambda i: (0, i)),
        out_shape=jax.ShapeDtypeStruct((bands, waves), jnp.float32),
        scratch_shapes=[
            pltpu.VMEM((rows, block), jnp.bfloat16),
            pltpu.VMEM((rows, block), jnp.bfloat16),
        ],
        compiler_params=params("arbitrary"),
        cost_estimate=pl.CostEstimate(
            flops=6 * waves * rows * bands, bytes_accessed=8 * waves * bands, transcendentals=0
        ),
        name="muffin",
    )(types, table, phase, sphere)


def sort_kernel(rank_ref, key_ref, wave_ref, send_ref, sorted_ref, rows_ref):
    waves, bands = wave_ref.shape
    parts, _, pairs, lanes = send_ref.shape
    half = lanes // 2

    def place(index, carry):
        target = rank_ref[index]
        rows_ref[pl.ds(target, 1), :] = wave_ref[pl.ds(index, 1), :]
        sorted_ref[target] = key_ref[index]
        return carry

    lax.fori_loop(0, waves, place, 0, unroll=8)

    def turn(tile, carry):
        start = pl.multiple_of(tile * lanes, lanes)
        turned = rows_ref[pl.ds(start, lanes), :].T
        for part in range(parts):
            first = part * 2 * pairs
            top = turned[first : first + pairs, :]
            low = turned[first + pairs : first + 2 * pairs, :]
            send_ref[part, 2 * tile] = jnp.concatenate([top[:, :half], low[:, :half]], axis=1)
            send_ref[part, 2 * tile + 1] = jnp.concatenate([top[:, half:], low[:, half:]], axis=1)
        return carry

    lax.fori_loop(0, waves // lanes, turn, 0)


def sort_call(rank, key, wave, parts, half):
    waves, bands = wave.shape
    pairs = bands // parts // 2
    return pl.pallas_call(
        sort_kernel,
        in_specs=[
            pl.BlockSpec(memory_space=pltpu.SMEM),
            pl.BlockSpec(memory_space=pltpu.SMEM),
            pl.BlockSpec(memory_space=pltpu.VMEM),
        ],
        out_specs=[
            pl.BlockSpec(memory_space=pltpu.VMEM),
            pl.BlockSpec(memory_space=pltpu.SMEM),
        ],
        out_shape=[
            jax.ShapeDtypeStruct((parts, waves // half, pairs, 2 * half), jnp.float32),
            jax.ShapeDtypeStruct((waves,), jnp.int32),
        ],
        scratch_shapes=[pltpu.VMEM((waves, bands), jnp.float32)],
        compiler_params=params(),
        name="sort",
    )(rank, key, wave)


def unsort_kernel(rank_ref, back_ref, wave_ref, kinetic_ref, out_ref, rows_ref):
    waves, bands = wave_ref.shape
    parts, _, pairs, lanes = back_ref.shape
    half = lanes // 2

    def turn(tile, carry):
        start = pl.multiple_of(tile * lanes, lanes)
        pieces = []
        for part in range(parts):
            even = back_ref[part, 2 * tile]
            odd = back_ref[part, 2 * tile + 1]
            pieces.append(jnp.concatenate([even[:, :half], odd[:, :half]], axis=1))
            pieces.append(jnp.concatenate([even[:, half:], odd[:, half:]], axis=1))
        rows_ref[pl.ds(start, lanes), :] = jnp.concatenate(pieces, axis=0).T
        return carry

    lax.fori_loop(0, waves // lanes, turn, 0)

    def place(index, carry):
        out_ref[pl.ds(index, 1), :] = rows_ref[pl.ds(rank_ref[index], 1), :]
        return carry

    lax.fori_loop(0, waves, place, 0, unroll=8)
    out_ref[...] += kinetic_ref[...] * wave_ref[...]


def unsort_call(rank, back, wave, kinetic):
    waves, bands = wave.shape
    vmem = pl.BlockSpec(memory_space=pltpu.VMEM)
    return pl.pallas_call(
        unsort_kernel,
        in_specs=[pl.BlockSpec(memory_space=pltpu.SMEM), vmem, vmem, vmem],
        out_specs=vmem,
        out_shape=jax.ShapeDtypeStruct((waves, bands), jnp.float32),
        scratch_shapes=[pltpu.VMEM((waves, bands), jnp.float32)],
        compiler_params=params(),
        name="unsort",
    )(rank, back, wave, kinetic[:, None])


def lane_gather(values, index):
    return jnp.take_along_axis(values, index, axis=1, mode="promise_in_bounds")


def grid_kernel(
    starts_ref,
    first_ref,
    last_ref,
    code_ref,
    slot_row_ref,
    slot_y_ref,
    potential_ref,
    left_ref,
    right_ref,
    compact_ref,
    out_ref,
    grid_ref,
    *,
    size,
    pitch,
    band_pitch,
):
    blocks, pairs, lanes = compact_ref.shape
    half = lanes // 2
    rows = size * size
    upper = lax.broadcasted_iota(jnp.int32, (pairs, lanes), 1) // half * half
    shift = int(math.log2(half))

    def expand_one(row):
        start = starts_ref[row]
        block = jnp.minimum(start >> shift, blocks - 1)
        following = jnp.minimum(block + 1, blocks - 1)
        code = jnp.broadcast_to(code_ref[pl.ds(row, 1), :], (pairs, lanes))
        place = code + (start & (half - 1))
        index = (place & (half - 1)) | upper
        here = lane_gather(compact_ref[block], index)
        there = lane_gather(compact_ref[following], index)
        value = jnp.where(place < half, here, there)
        value = jnp.where(code >= 0, value, 0.0)
        target = (row // size) * pitch + row % size
        grid_ref[pl.ds(target, pairs, stride=band_pitch), :] = value

    def expand(group, carry):
        for step in range(8):
            expand_one(group * 8 + step)
        return carry

    lax.fori_loop(0, rows // 8, expand, 0)

    left = left_ref[...]
    right = right_ref[...]

    def apply_left(value):
        high, low = split_bf16(value)
        both = dot32(left, jnp.concatenate([high, low], axis=0))
        return both[:size, :] + both[size:, :]

    def apply_right(value):
        high, low = split_bf16(value)
        both = dot32(jnp.concatenate([high, low], axis=1), right)
        return both[:, :lanes] + both[:, lanes:]

    many = 8

    def planes(turn, carry):
        pair = turn // (size // many)
        base = pair * band_pitch + (turn % (size // many)) * many * pitch
        starts = [pl.multiple_of(base + index * pitch, 8) for index in range(many)]
        field = jnp.concatenate([grid_ref[pl.ds(s, size), :] for s in starts], axis=1)
        field = apply_left(field)
        field = jnp.concatenate(
            [field[:, index * lanes : (index + 1) * lanes] for index in range(many)], axis=0
        )
        field = apply_right(field)
        for index, s in enumerate(starts):
            grid_ref[pl.ds(s, size), :] = field[index * size : (index + 1) * size, :]
        return carry

    def columns(turn, carry):
        pair = turn // (size // many)
        along = (turn % (size // many)) * many
        base = pair * band_pitch + along
        field = jnp.concatenate(
            [grid_ref[pl.ds(base + index, size, stride=pitch), :] for index in range(many)], axis=1
        )
        field = apply_left(field)
        weight = jnp.concatenate(
            [
                potential_ref[pl.ds(pl.multiple_of((along + index) * size, size), size), :]
                for index in range(many)
            ],
            axis=1,
        )
        field = apply_left(field * weight)
        for index in range(many):
            grid_ref[pl.ds(base + index, size, stride=pitch), :] = field[
                :, index * lanes : (index + 1) * lanes
            ]
        return carry

    turns = pairs * (size // many)
    lax.fori_loop(0, turns, planes, 0)
    lax.fori_loop(0, turns, columns, 0)
    lax.fori_loop(0, turns, planes, 0)

    def collect(block, carry):
        wanted = jnp.broadcast_to(slot_row_ref[pl.ds(block, 1), :], (pairs, lanes))
        index = jnp.broadcast_to(slot_y_ref[pl.ds(block, 1), :], (pairs, lanes))
        first = first_ref[block]
        trips = (last_ref[block] - first) // many + 1

        def some(trip, value):
            for step in range(many):
                row = jnp.minimum(first + trip * many + step, rows - 1)
                source = (row // size) * pitch + row % size
                here = lane_gather(grid_ref[pl.ds(source, pairs, stride=band_pitch), :], index)
                value = jnp.where(wanted == row, here, value)
            return value

        out_ref[block] = lax.fori_loop(0, trips, some, jnp.zeros((pairs, lanes), jnp.float32))
        return carry

    lax.fori_loop(0, blocks, collect, 0)


def grid_call(starts, first, last, code, slot_row, slot_y, potential, left, right, compact, size):
    blocks, pairs, lanes = compact.shape
    pitch = size + 8
    band_pitch = size * pitch + 8
    smem = pl.BlockSpec(memory_space=pltpu.SMEM)
    vmem = pl.BlockSpec(memory_space=pltpu.VMEM)
    points = 2 * pairs * size**3
    return pl.pallas_call(
        functools.partial(grid_kernel, size=size, pitch=pitch, band_pitch=band_pitch),
        in_specs=[smem] * 3 + [vmem] * 7,
        out_specs=vmem,
        out_shape=jax.ShapeDtypeStruct(compact.shape, jnp.float32),
        scratch_shapes=[pltpu.VMEM((pairs * band_pitch, lanes), jnp.float32)],
        compiler_params=params(),
        cost_estimate=pl.CostEstimate(
            flops=36 * size * points, bytes_accessed=4 * points, transcendentals=0
        ),
        name="grid",
    )(starts, first, last, code, slot_row, slot_y, potential, left, right, compact)


def finish_kernel(muffin_ref, rest_ref, all_ref, out_ref, sub_ref):
    bands = out_ref.shape[1]

    @pl.when(pl.program_id(0) == 0)
    def _():
        sub_ref[...] = jnp.zeros_like(sub_ref)

    applied = muffin_ref[...] + rest_ref[...].T
    out_ref[...] = applied.T
    high, low = split_bf16(applied)
    all_high, all_low = split_bf16(all_ref[...])
    main = dot32(jnp.concatenate([high, low], axis=0), all_high)
    sub_ref[...] += main[:bands, :] + main[bands:, :] + dot32(high, all_low)


def finish_call(muffin, rest, columns):
    waves, bands = rest.shape
    total = columns.shape[1]
    block = math.gcd(waves, 512)
    return pl.pallas_call(
        finish_kernel,
        grid=(waves // block,),
        in_specs=[
            pl.BlockSpec((bands, block), lambda i: (0, i)),
            pl.BlockSpec((block, bands), lambda i: (i, 0)),
            pl.BlockSpec((block, total), lambda i: (i, 0)),
        ],
        out_specs=[
            pl.BlockSpec((block, bands), lambda i: (i, 0)),
            pl.BlockSpec((bands, total), lambda i: (0, 0)),
        ],
        out_shape=[
            jax.ShapeDtypeStruct((waves, bands), jnp.float32),
            jax.ShapeDtypeStruct((bands, total), jnp.float32),
        ],
        compiler_params=params("arbitrary"),
        name="finish",
    )(muffin, rest, columns)


def exchange(array):
    return lax.all_to_all(array, "pw", split_axis=0, concat_axis=0, tiled=True)


def round_high(value):
    return lax.reduce_precision(value, 8, 7)


def interstitial_tables(size):
    table = cas_matrix(size)
    high = round_high(table)
    low = round_high(table - high)
    zero = jnp.zeros_like(table)
    left = jnp.concatenate(
        [jnp.concatenate([high, high], axis=1), jnp.concatenate([low, zero], axis=1)], axis=0
    )

    def twice(block):
        return jnp.concatenate(
            [jnp.concatenate([block, zero], axis=1), jnp.concatenate([zero, block], axis=1)], axis=0
        )

    right = jnp.concatenate(
        [
            jnp.concatenate([twice(high), twice(low)], axis=1),
            jnp.concatenate([twice(high), jnp.zeros((2 * size, 2 * size))], axis=1),
        ],
        axis=0,
    )
    return left.astype(jnp.bfloat16), right.astype(jnp.bfloat16)


def per_device(wave_coeffs, miller, atom_types, positions, sphere_radii, h_blocks, potential):
    pw_count = lax.axis_size("pw")
    pw_index = lax.axis_index("pw")
    local_waves, local_bands = wave_coeffs.shape
    size = potential.shape[1]
    kinds, funcs_each = h_blocks.shape[:2]
    atom_total = atom_types.shape[0]
    factor = NPW ** (-0.5)
    miller_float = miller.astype(jnp.float32)
    kinetic = jnp.sum(miller_float * miller_float, axis=0) / 1536.0
    planes_each = size // pw_count
    lines = planes_each * size

    wrapped = jnp.mod(miller, size)
    line = (wrapped[2] - pw_index * planes_each) * size + wrapped[0]
    key = line * size + wrapped[1]
    rank = jnp.sum((key[:, None] < key[None, :]).astype(jnp.int32), axis=0)
    starts = jnp.sum(
        (line[:, None] < jnp.arange(lines, dtype=jnp.int32)[None, :]).astype(jnp.int32), axis=0
    )
    line_onehot = (line[None, :] == jnp.arange(lines, dtype=jnp.int32)[:, None]).astype(
        jnp.bfloat16
    )
    across = jnp.arange(size, dtype=jnp.int32)
    y_onehot = (wrapped[1][:, None] == across[None, :]).astype(jnp.bfloat16)
    filled = jnp.dot(line_onehot, y_onehot, preferred_element_type=jnp.float32)
    before = (across[:, None] < across[None, :]).astype(jnp.bfloat16)
    ahead = jnp.dot(filled.astype(jnp.bfloat16), before, preferred_element_type=jnp.float32)
    code = jnp.where(filled > 0.5, ahead, -1024.0)

    send, sorted_key = sort_call(rank, key, wave_coeffs, pw_count, size)
    turned = jnp.transpose(potential, (0, 2, 1))
    pieces = [
        turned.reshape(-1),
        code.reshape(-1),
        starts.astype(jnp.float32),
        sorted_key.astype(jnp.float32),
    ]
    cuts = np.cumsum([piece.shape[0] for piece in pieces])
    known = lax.all_gather(jnp.concatenate(pieces), "pw", axis=0, tiled=False)
    compact = exchange(send)

    spheres, matching_table, phase = sphere_call(
        atom_types, miller, positions, sphere_radii, wave_coeffs, kinds, funcs_each, 2.0 / size
    )
    atoms_each = atom_total // pw_count
    parts = exchange(spheres.reshape(pw_count, atoms_each * funcs_each, local_bands))
    mine = jnp.sum(parts, axis=0).reshape(atoms_each, funcs_each, local_bands)
    own_types = lax.dynamic_slice_in_dim(atom_types, pw_index * atoms_each, atoms_each, 0)
    own_onehot = (own_types[:, None] == jnp.arange(kinds, dtype=jnp.int32)[None, :]).astype(
        jnp.float32
    )
    chosen = jnp.einsum("at,tfk->afk", own_onehot, h_blocks, precision=PRECISE)
    applied = jnp.einsum("akb,afk->baf", mine, chosen, precision=PRECISE).reshape(
        1, local_bands, atoms_each * funcs_each
    )
    applied = exchange(jnp.broadcast_to(applied, (pw_count,) + applied.shape[1:]))
    applied = jnp.transpose(applied, (1, 0, 2)).reshape(local_bands, atom_total * funcs_each)

    wave_again, known = lax.optimization_barrier((wave_coeffs, known))
    columns = lax.all_gather(wave_again, "band", axis=1, tiled=True)

    field = known[:, : cuts[0]].reshape(size * size, size)
    field = jnp.concatenate([field, field], axis=1)
    codes = known[:, cuts[0] : cuts[1]].reshape(size * size, size).astype(jnp.int32)
    codes = jnp.concatenate([codes, codes], axis=1)
    offsets = jnp.arange(pw_count, dtype=jnp.int32)[:, None]
    all_starts = known[:, cuts[1] : cuts[2]].astype(jnp.int32) + offsets * local_waves
    all_keys = known[:, cuts[2] : cuts[3]].astype(jnp.int32)
    all_keys = (all_keys + offsets * (lines * size)).reshape(-1, size)
    slot_row = all_keys // size
    slot_y = all_keys % size
    left, right = interstitial_tables(size)
    back = grid_call(
        all_starts.reshape(-1),
        slot_row[:, 0],
        slot_row[:, -1],
        codes,
        jnp.concatenate([slot_row, slot_row], axis=1),
        jnp.concatenate([slot_y, slot_y + size], axis=1),
        field,
        left,
        right,
        compact.reshape(-1, *compact.shape[2:]),
        size,
    )
    back = exchange(back.reshape(compact.shape))
    muffin = muffin_call(atom_types, matching_table, phase, applied)
    rest = unsort_call(rank, back, wave_coeffs, kinetic)
    h_applied, partial = finish_call(muffin, rest, columns)
    partial = jnp.transpose(partial) * factor
    rows_each = partial.shape[0] // pw_count
    gathered = exchange(partial.reshape(pw_count, rows_each, local_bands))
    return (h_applied, jnp.sum(gathered, axis=0))


def solution(mesh):
    in_specs = (P("pw", "band"), P(None, "pw"), P(), P(), P(), P(), P("pw", None, None))
    out_specs = (P("pw", "band"), P("pw", "band"))
    return jax.shard_map(
        per_device, mesh=mesh, in_specs=in_specs, out_specs=out_specs, check_vma=False
    )
```

time: 1500 us -> 512 us (0.34)
  matrix products: 852 us -> 2.82 us
  waiting for transfers between devices: 493 us -> 100 us
  Pallas kernels: 0 us -> 321 us
  local copies, waits for them, and re-layouts: 101 us -> 16.8 us
    dot_general x65 -> x4, matrix products: 852 us -> 2.82 us  [the longest x1 2.03 us: per_device(): filled = jnp.dot(line_onehot, y_onehot, preferred_element_type=jnp.float32)]
    pallas_call x0 -> x6, Pallas kernels: none -> 321 us  [the longest x1 236 us: grid_call(): pl.pallas_call(functools.partial(grid_kernel, size=size, pitch=pitch, ban...]
    all_to_all x2 -> x4, waiting for transfers between devices: 354 us -> 100 us  [exchange(): return lax.all_to_all(array, 'pw', split_axis=0, concat_axis=0, tiled=True)]
    psum x1 -> x0, waiting for transfers between devices: 76.9 us -> none  [per_device(): lax.psum(lax.map(one_block, jnp.arange(count // width, dtype=jnp.int32))....]
    unnamed x4 -> x2, waiting for transfers between devices: 62.4 us -> 0.03 us
    all_to_all x2 -> x0, local copies, waits for them, and re-layouts: 23.6 us -> none  [the longest x1 11.8 us: per_device(): lax.all_to_all(back_field, 'pw', split_axis=0, concat_axis=1, tiled=True)]
    gather x1 -> x0, local copies, waits for them, and re-layouts: 20.1 us -> none  [per_device(): slab_grid.reshape(planes_each * grid_size * grid_size, local_bands)]
    dot_general x1 -> x0, local copies, waits for them, and re-layouts: 19.3 us -> none  [per_device(): back_field = jnp.einsum('cz,zxyb->cxyb', table, weighted, precision=PRECISE)]
  transfers between devices with their start and end apart: 5 -> 6, of which waited for: 3 -> 3; matrix products, arithmetic and copies ran while one was open for 52% -> 5% of each run, Pallas kernels for 0% -> 58%
where the time goes in v1:
time: 512 us; the launch traced here: 511 us
  Pallas kernels  321 us (63%)
  waiting for transfers between devices  100 us (20%)
  other arithmetic  22.2 us (4%)
  starting transfers between devices  21.5 us (4%)
  local copies, waits for them, and re-layouts  16.8 us (3%)
  between operations  14.3 us (3%)
  blocking collectives  12.5 us (2%)
    pallas_call x1, Pallas kernels, grid_call(): pl.pallas_call(functools.partial(grid_kernel, size=size, pitch=pitch, ban...  236 us
    all_to_all x4, waiting for transfers between devices, exchange(): return lax.all_to_all(array, 'pw', split_axis=0, concat_axis=0, tiled=True)  100 us
    pallas_call x1, Pallas kernels, sphere_call(): pl.pallas_call(functools.partial(sphere_kernel, spacing=spacing), grid=(w...  26.2 us
    all_to_all x4, starting transfers between devices, exchange(): return lax.all_to_all(array, 'pw', split_axis=0, concat_axis=0, tiled=True)  21.4 us
    pallas_call x1, Pallas kernels, muffin_call(): pl.pallas_call(muffin_kernel, grid=(waves // block,), in_specs=[pl.BlockS...  17.4 us
    pallas_call x1, Pallas kernels, sort_call(): pl.pallas_call(sort_kernel, in_specs=[pl.BlockSpec(memory_space=pltpu.SME...  16.5 us
    pallas_call x1, Pallas kernels, unsort_call(): pl.pallas_call(unsort_kernel, in_specs=[pl.BlockSpec(memory_space=pltpu.S...  15.5 us
    all_to_all x1, blocking collectives, exchange(): return lax.all_to_all(array, 'pw', split_axis=0, concat_axis=0, tiled=True)  12.5 us
  transfers between devices with their start and end apart: 6, of which 3 were waited for; matrix products, arithmetic and copies ran while one was open for 5% of the time, Pallas kernels for 58%

profile of v1, /device:TPU:0, one launch (start us, length us, event | category | flops | bytes accessed | tf_op | source)
XLA Modules:
  0.0 511.3 jit_solution(4793463044831135689)
XLA Ops:
  7.2 0.9 add_select_fusion.2
  8.2 1.0 convert_reduce_fusion.1
  9.2 2.0 fusion
  11.3 8.9 %convert_reduce_fusion.rank_ref = s32[4096]{0:T(1024)} fusion(s32[4096]{0:T(1024)S(1)} %bitcast.49, s32[4096]{0:T(1024)S(1)} %multiply_add_fusion.1.key_ref), kind=kLoop, calls=%fused_computation | loop fusion | flops 50327552 | bytes 49152 | tf_op jit(solution)/shard_map/reduce_sum | solution.py:575
  20.2 16.5 %sort.1 = (f32[8,64,8,128]{3,2,1,0:T(8,128)}, s32[4096]{0:T(1024)}) custom-call(s32[4096]{0:T(1024)} %convert_reduce_fusion.rank_ref, s32[4096]{0:T(1024)} %copy-done.7, f32[4096,128]{1,0:T(8,128)} %wave_ref.5), custom_call_target="tpu_custom_call" | custom-call | tf_op jit(solution)/shard_map/sort/pallas_call | solution.py:280
  36.7 0.7 convert_element_type.53
  37.4 0.2 convolution_select_fusion
  38.2 0.9 reshape.102
  39.1 0.7 copy.29
  39.8 0.7 copy.30.radii_ref
  40.5 26.2 %sphere.1 = (f32[2048,128]{1,0:T(8,128)}, f32[4,64,4096]{2,1,0:T(8,128)}, f32[32,4096]{1,0:T(8,128)}) custom-call(s32[32]{0:T(128)} %types_ref.3, s32[3,4096]{1,0:T(4,128)} %miller_ref.1, f32[32,3]{1,0:T(8,128)} %bitcast.47, f32[4,1]{1,0:T(4,128)} %copy.30.radii_ref, f32[4096,128]{1,0:T(8,128)} %wave_ref.5), custom_call_target="tpu_custom_call" | custom-call | flops 6442450944 | bytes 4194304 | tf_op jit(solution)/shard_map/sphere/pallas_call | solution.py:180
  66.7 7.3 %all-to-all-start = ((f32[8,256,128]{2,1,0:T(8,128)}), f32[8,256,128]{2,1,0:T(8,128)S(1)}, u32[]{:S(2)}, u32[]{:S(2)}) async-start(f32[8,256,128]{2,1,0:T(8,128)} %bitcast.35), calls=%async_computation | async-start | bytes 2097152 | tf_op jit(solution)/shard_map/all_to_all | solution.py:528
  74.1 0.2 subtract_reduce-precision_fusion
  74.3 0.2 fusion.28
  74.4 0.2 fusion.27
  74.6 0.2 fusion.29
  74.9 0.7 pad_maximum_fusion.2.left_ref
  75.6 0.7 fusion.12.right_ref
  76.3 0.3 fusion.15
  76.6 36.1 %all-to-all-done = f32[8,256,128]{2,1,0:T(8,128)S(1)} async-done(((f32[8,256,128]{2,1,0:T(8,128)}), f32[8,256,128]{2,1,0:T(8,128)S(1)}, u32[]{:S(2)}, u32[]{:S(2)}) %all-to-all-start) | async-done | bytes 1048608 | tf_op jit(solution)/shard_map/all_to_all | solution.py:528
  112.7 4.4 all-to-all-start.2
  117.2 0.3 fusion.13
  117.4 0.8 copy.33
  118.2 1.8 copy.47
  120.0 1.4 fusion.33
  121.5 0.6 copy.41
  122.3 2.1 convert_element_type.57
  124.4 2.1 reshape.97
  126.6 0.2 broadcast_add_fusion
  126.8 0.9 slice_reduce_fusion
  127.7 1.0 pad_add_fusion.1
  128.7 36.9 %all-to-all-done.2 = f32[8,64,8,128]{3,2,1,0:T(8,128)} async-done(((f32[8,64,8,128]{3,2,1,0:T(8,128)}), f32[8,64,8,128]{3,2,1,0:T(8,128)}, u32[]{:S(2)}, u32[]{:S(2)}) %all-to-all-start.2) | async-done | bytes 2097184 | tf_op jit(solution)/shard_map/all_to_all | solution.py:528
  165.6 1.1 broadcast_in_dim.11
  166.7 3.7 all-to-all-start.1
  170.5 1.9 pad_add_fusion.code_ref
  172.4 1.9 pad_maximum_fusion.potential_ref
  174.3 236.2 %grid.1 = f32[512,8,128]{2,1,0:T(8,128)} custom-call(s32[4096]{0:T(1024)} %bitcast.48, s32[512]{0:T(512)} %get-tuple-element.21.first_ref, s32[512]{0:T(512)} %get-tuple-element.20.last_ref, s32[4096,128]{1,0:T(8,128)} %pad_add_fusion.code_ref, s32[512,128]{1,0:T(8,128)} %get-tuple-element.30.slot_row_ref, s32[512,128]{1,0:T(8,128)} %get-tuple-element.31.slot_y_ref, ...), custom_call_target="tpu_custom_call" | custom-call | flops 9663676416 | bytes 16777216 | tf_op jit(solution)/shard_map/grid/pallas_call | solution.py:473
  410.6 6.0 %all-to-all-start.3 = ((f32[8,64,8,128]{3,2,1,0:T(8,128)}), f32[8,64,8,128]{3,2,1,0:T(8,128)S(1)}, u32[]{:S(2)}, u32[]{:S(2)}) async-start(f32[8,64,8,128]{3,2,1,0:T(8,128)} %bitcast.34), calls=%async_computation.3 | async-start | bytes 4194304 | tf_op jit(solution)/shard_map/all_to_all | solution.py:528
  416.6 2.0 copy.37.kinetic_ref
  418.6 1.1 copy.40
  419.7 17.4 %muffin.1.muffin_ref = f32[128,4096]{1,0:T(8,128)} custom-call(s32[32]{0:T(128)} %types_ref.3, f32[4,64,4096]{2,1,0:T(8,128)} %get-tuple-element.11.table_ref, f32[32,4096]{1,0:T(8,128)} %get-tuple-element.12.phase_ref, f32[128,2048]{1,0:T(8,128)} %bitcast.36), custom_call_target="tpu_custom_call" | custom-call | flops 6442450944 | bytes 4194304 | tf_op jit(solution)/shard_map/muffin/pallas_call | solution.py:227
  437.1 27.3 %all-to-all-done.3.back_ref = f32[8,64,8,128]{3,2,1,0:T(8,128)S(1)} async-done(((f32[8,64,8,128]{3,2,1,0:T(8,128)}), f32[8,64,8,128]{3,2,1,0:T(8,128)S(1)}, u32[]{:S(2)}, u32[]{:S(2)}) %all-to-all-start.3) | async-done | bytes 2097184 | tf_op jit(solution)/shard_map/all_to_all | solution.py:528
  464.4 1.3 copy-done.2
  465.7 15.5 %unsort.1.rest_ref = f32[4096,128]{1,0:T(8,128)} custom-call(s32[4096]{0:T(1024)} %convert_reduce_fusion.rank_ref, f32[8,64,8,128]{3,2,1,0:T(8,128)} %copy-done.2, f32[4096,128]{1,0:T(8,128)} %wave_ref.5, f32[4096,1]{1,0:T(8,128)} %copy.37.kinetic_ref), custom_call_target="tpu_custom_call" | custom-call | tf_op jit(solution)/shard_map/unsort/pallas_call | solution.py:330
  481.3 8.9 %finish.1 = (f32[4096,128]{1,0:T(8,128)}, f32[128,512]{1,0:T(8,128)}) custom-call(f32[128,4096]{1,0:T(8,128)} %muffin.1.muffin_ref, f32[4096,128]{1,0:T(8,128)} %unsort.1.rest_ref, f32[4096,512]{1,0:T(8,128)} %all-gather.5.cloned.1.call-done.all_ref), custom_call_target="tpu_custom_call" | custom-call | tf_op jit(solution)/shard_map/finish/pallas_call | solution.py:506
  490.2 1.0 multiply_bitcast_fusion
  491.3 12.5 %all_to_all.25 = f32[8,64,128]{2,1,0:T(8,128)S(1)} all-to-all(f32[8,64,128]{2,1,0:T(8,128)S(1)} %bitcast.37), channel_id=1, replica_groups=mesh['band'=4,'pw'=8] {'pw'}, dimensions={0} | all-to-all | bytes 524288 | tf_op jit(solution)/shard_map/all_to_all | solution.py:528
  503.9 0.6 reduce_sum.49
  (48 shorter events, 1.4 us)
Async XLA Ops:
  7.2 69.1 %copy-start = (f32[4,64,64]{2,1,0:T(8,128)S(1)}, f32[4,64,64]{2,1,0:T(8,128)}, u32[]{:S(2)}) copy-start(f32[4,64,64]{2,1,0:T(8,128)} %param.12) | copy-start | bytes 196612
  7.2 111.0 %all-gather.7.cloned.1.call-start = ((), (), s32[]{:S(2)}) async-start(), calls=%async_computation.6 | async-start | bytes 2525184 | tf_op jit(solution)/shard_map/all_gather | solution.py:598
  9.2 2.0 copy-start.7
  11.2 26.6 %copy-start.6 = (f32[8,64,64]{2,1,0:T(8,128)S(1)}, f32[8,64,64]{2,1,0:T(8,128)}, u32[]{:S(2)}) copy-start(f32[8,64,64]{2,1,0:T(8,128)} %param.13) | copy-start | bytes 393220
  36.7 2.4 copy-start.8
  36.7 3.1 copy-start.9
  66.7 7.3 %copy-start.10 = (s32[32]{0:T(128)S(1)}, s32[32]{0:T(128)}, u32[]{:S(2)}) copy-start(s32[32]{0:T(128)} %types_ref.3) | copy-start | bytes 388
  66.7 46.0 %all-to-all-start = ((f32[8,256,128]{2,1,0:T(8,128)}), f32[8,256,128]{2,1,0:T(8,128)S(1)}, u32[]{:S(2)}, u32[]{:S(2)}) async-start(f32[8,256,128]{2,1,0:T(8,128)} %bitcast.35), calls=%async_computation | async-start | bytes 2097152 | tf_op jit(solution)/shard_map/all_to_all | solution.py:528
  112.7 53.0 %all-to-all-start.2 = ((f32[8,64,8,128]{3,2,1,0:T(8,128)}), f32[8,64,8,128]{3,2,1,0:T(8,128)}, u32[]{:S(2)}, u32[]{:S(2)}) async-start(f32[8,64,8,128]{3,2,1,0:T(8,128)} %get-tuple-element.16), calls=%async_computation.2 | async-start | bytes 4194304 | tf_op jit(solution)/shard_map/all_to_all | solution.py:528
  117.0 364.2 %all-gather.5.cloned.1.call-start = ((), (), s32[]{:S(2)}) async-start(), calls=%async_computation.5 | async-start | bytes 10485760 | tf_op jit(solution)/shard_map/all_gather | solution.py:619
  122.2 2.2 copy-start.3
  126.6 39.1 %copy-start.4 = (f32[128,256]{1,0:T(8,128)S(1)}, f32[128,256]{1,0:T(8,128)}, u32[]{:S(2)}) copy-start(f32[128,256]{1,0:T(8,128)} %copy.33) | copy-start | bytes 393220
  166.7 243.9 %all-to-all-start.1 = ((f32[8,128,256]{2,1,0:T(8,128)}), f32[8,128,256]{2,1,0:T(8,128)S(1)}, u32[]{:S(2)}, u32[]{:S(2)}) async-start(f32[8,128,256]{2,1,0:T(8,128)} %broadcast_in_dim.11), calls=%async_computation.1 | async-start | bytes 2097152 | tf_op jit(solution)/shard_map/all_to_all | solution.py:528
  170.4 1.9 copy-start.1
  410.6 6.0 %copy-start.5 = (s32[3,4096]{1,0:T(4,128)S(1)}, s32[3,4096]{1,0:T(4,128)}, u32[]{:S(2)}) copy-start(s32[3,4096]{1,0:T(4,128)} %miller_ref.1) | copy-start | bytes 147460
  410.6 53.9 %all-to-all-start.3 = ((f32[8,64,8,128]{3,2,1,0:T(8,128)}), f32[8,64,8,128]{3,2,1,0:T(8,128)S(1)}, u32[]{:S(2)}, u32[]{:S(2)}) async-start(f32[8,64,8,128]{3,2,1,0:T(8,128)} %bitcast.34), calls=%async_computation.3 | async-start | bytes 4194304 | tf_op jit(solution)/shard_map/all_to_all | solution.py:528
  464.4 1.3 copy-start.2
Sparse Core Ops, SparseCore 0:
  39.2 71.1 all-gather.6
  120.1 60.6 all-gather.4

commit v2 on v1

--- a/solution.py
+++ b/solution.py
@@ -210,16 +210,27 @@
     )(types, miller, positions.T, radii[:, None], wave)
 
 
-def muffin_kernel(types_ref, table_ref, phase_ref, sphere_ref, out_ref, high_ref, low_ref):
+def muffin_kernel(
+    types_ref,
+    table_ref,
+    phase_ref,
+    sphere_ref,
+    kinetic_ref,
+    wave_ref,
+    out_ref,
+    high_ref,
+    low_ref,
+):
     bands = out_ref.shape[0]
     fill_matching(types_ref, table_ref, phase_ref, high_ref, low_ref)
     high, low = split_bf16(sphere_ref[...])
     main = dot32(jnp.concatenate([high, low], axis=0), high_ref[...])
     rest = dot32(high, low_ref[...])
-    out_ref[...] = main[:bands, :] + main[bands:, :] + rest
-
-
-def muffin_call(types, table, phase, sphere):
+    kinetic = kinetic_ref[...] * wave_ref[...].T
+    out_ref[...] = main[:bands, :] + main[bands:, :] + rest + kinetic
+
+
+def muffin_call(types, table, phase, sphere, kinetic, wave):
     kinds, funcs, waves = table.shape
     atoms = phase.shape[0]
     bands, rows = sphere.shape
@@ -232,6 +243,8 @@
             pl.BlockSpec((kinds, funcs, block), lambda i: (0, 0, i)),
             pl.BlockSpec((atoms, block), lambda i: (0, i)),
             pl.BlockSpec((bands, rows), lambda i: (0, 0)),
+            pl.BlockSpec((1, block), lambda i: (0, i)),
+            pl.BlockSpec((block, bands), lambda i: (i, 0)),
         ],
         out_specs=pl.BlockSpec((bands, block), lambda i: (0, i)),
         out_shape=jax.ShapeDtypeStruct((bands, waves), jnp.float32),
@@ -244,11 +257,11 @@
             flops=6 * waves * rows * bands, bytes_accessed=8 * waves * bands, transcendentals=0
         ),
         name="muffin",
-    )(types, table, phase, sphere)
+    )(types, table, phase, sphere, kinetic[None, :], wave)
 
 
 def sort_kernel(rank_ref, key_ref, wave_ref, send_ref, sorted_ref, rows_ref):
-    waves, bands = wave_ref.shape
+    waves, _ = wave_ref.shape
     parts, _, pairs, lanes = send_ref.shape
     half = lanes // 2
 
@@ -258,7 +271,7 @@
         sorted_ref[target] = key_ref[index]
         return carry
 
-    lax.fori_loop(0, waves, place, 0, unroll=8)
+    lax.fori_loop(0, waves, place, 0, unroll=32)
 
     def turn(tile, carry):
         start = pl.multiple_of(tile * lanes, lanes)
@@ -298,52 +311,25 @@
     )(rank, key, wave)
 
 
-def unsort_kernel(rank_ref, back_ref, wave_ref, kinetic_ref, out_ref, rows_ref):
-    waves, bands = wave_ref.shape
-    parts, _, pairs, lanes = back_ref.shape
-    half = lanes // 2
-
-    def turn(tile, carry):
-        start = pl.multiple_of(tile * lanes, lanes)
-        pieces = []
-        for part in range(parts):
-            even = back_ref[part, 2 * tile]
-            odd = back_ref[part, 2 * tile + 1]
-            pieces.append(jnp.concatenate([even[:, :half], odd[:, :half]], axis=1))
-            pieces.append(jnp.concatenate([even[:, half:], odd[:, half:]], axis=1))
-        rows_ref[pl.ds(start, lanes), :] = jnp.concatenate(pieces, axis=0).T
-        return carry
-
-    lax.fori_loop(0, waves // lanes, turn, 0)
-
-    def place(index, carry):
-        out_ref[pl.ds(index, 1), :] = rows_ref[pl.ds(rank_ref[index], 1), :]
-        return carry
-
-    lax.fori_loop(0, waves, place, 0, unroll=8)
-    out_ref[...] += kinetic_ref[...] * wave_ref[...]
-
-
-def unsort_call(rank, back, wave, kinetic):
-    waves, bands = wave.shape
-    vmem = pl.BlockSpec(memory_space=pltpu.VMEM)
-    return pl.pallas_call(
-        unsort_kernel,
-        in_specs=[pl.BlockSpec(memory_space=pltpu.SMEM), vmem, vmem, vmem],
-        out_specs=vmem,
-        out_shape=jax.ShapeDtypeStruct((waves, bands), jnp.float32),
-        scratch_shapes=[pltpu.VMEM((waves, bands), jnp.float32)],
-        compiler_params=params(),
-        name="unsort",
-    )(rank, back, wave, kinetic[:, None])
-
-
 def lane_gather(values, index):
-    return jnp.take_along_axis(values, index, axis=1, mode="promise_in_bounds")
+    numbers = lax.GatherDimensionNumbers(
+        offset_dims=(),
+        collapsed_slice_dims=(1,),
+        start_index_map=(1,),
+        operand_batching_dims=(0,),
+        start_indices_batching_dims=(0,),
+    )
+    return lax.gather(
+        values,
+        index[..., None],
+        numbers,
+        slice_sizes=(1, 1),
+        mode=lax.GatherScatterMode.PROMISE_IN_BOUNDS,
+    )
 
 
 def grid_kernel(
-    starts_ref,
+    block_ref,
     first_ref,
     last_ref,
     code_ref,
@@ -360,32 +346,30 @@
     pitch,
     band_pitch,
 ):
-    blocks, pairs, lanes = compact_ref.shape
+    blocks, pairs, lanes = out_ref.shape
     half = lanes // 2
     rows = size * size
+    shift = size.bit_length() - 1
+    extra = pitch - size
     upper = lax.broadcasted_iota(jnp.int32, (pairs, lanes), 1) // half * half
-    shift = int(math.log2(half))
-
-    def expand_one(row):
-        start = starts_ref[row]
-        block = jnp.minimum(start >> shift, blocks - 1)
-        following = jnp.minimum(block + 1, blocks - 1)
-        code = jnp.broadcast_to(code_ref[pl.ds(row, 1), :], (pairs, lanes))
-        place = code + (start & (half - 1))
-        index = (place & (half - 1)) | upper
-        here = lane_gather(compact_ref[block], index)
-        there = lane_gather(compact_ref[following], index)
-        value = jnp.where(place < half, here, there)
-        value = jnp.where(code >= 0, value, 0.0)
-        target = (row // size) * pitch + row % size
-        grid_ref[pl.ds(target, pairs, stride=band_pitch), :] = value
+    wide = math.gcd(rows, 64)
 
     def expand(group, carry):
-        for step in range(8):
-            expand_one(group * 8 + step)
+        base = group * wide
+        place = base + lax.shift_right_logical(base, shift) * extra
+        for step in range(wide):
+            row = base + step
+            block = block_ref[row]
+            code = jnp.broadcast_to(code_ref[pl.ds(row, 1), :], (pairs, lanes))
+            index = (code & (half - 1)) | upper
+            here = lane_gather(compact_ref[block], index)
+            there = lane_gather(compact_ref[block + 1], index)
+            value = jnp.where(code < half, here, there)
+            value = jnp.where(code >= 0, value, 0.0)
+            grid_ref[pl.ds(place + step, pairs, stride=band_pitch), :] = value
         return carry
 
-    lax.fori_loop(0, rows // 8, expand, 0)
+    lax.fori_loop(0, rows // wide, expand, 0)
 
     left = left_ref[...]
     right = right_ref[...]
@@ -402,69 +386,102 @@
 
     many = 8
 
+    chains = max(1, math.gcd(size // many, 4))
+    groups = size // (many * chains)
+
     def planes(turn, carry):
-        pair = turn // (size // many)
-        base = pair * band_pitch + (turn % (size // many)) * many * pitch
-        starts = [pl.multiple_of(base + index * pitch, 8) for index in range(many)]
-        field = jnp.concatenate([grid_ref[pl.ds(s, size), :] for s in starts], axis=1)
-        field = apply_left(field)
-        field = jnp.concatenate(
-            [field[:, index * lanes : (index + 1) * lanes] for index in range(many)], axis=0
-        )
-        field = apply_right(field)
-        for index, s in enumerate(starts):
-            grid_ref[pl.ds(s, size), :] = field[index * size : (index + 1) * size, :]
+        base = turn // groups * band_pitch
+        offset = turn % groups * (many * chains * pitch)
+        for chain in range(chains):
+            starts = [
+                pl.multiple_of(base + offset + (chain * many + index) * pitch, 8)
+                for index in range(many)
+            ]
+            field = jnp.concatenate([grid_ref[pl.ds(s, size), :] for s in starts], axis=1)
+            field = apply_left(field)
+            field = jnp.concatenate(
+                [field[:, index * lanes : (index + 1) * lanes] for index in range(many)], axis=0
+            )
+            field = apply_right(field)
+            for index, s in enumerate(starts):
+                grid_ref[pl.ds(s, size), :] = field[index * size : (index + 1) * size, :]
         return carry
 
     def columns(turn, carry):
-        pair = turn // (size // many)
-        along = (turn % (size // many)) * many
-        base = pair * band_pitch + along
-        field = jnp.concatenate(
-            [grid_ref[pl.ds(base + index, size, stride=pitch), :] for index in range(many)], axis=1
-        )
-        field = apply_left(field)
-        weight = jnp.concatenate(
-            [
-                potential_ref[pl.ds(pl.multiple_of((along + index) * size, size), size), :]
-                for index in range(many)
-            ],
-            axis=1,
-        )
-        field = apply_left(field * weight)
-        for index in range(many):
-            grid_ref[pl.ds(base + index, size, stride=pitch), :] = field[
-                :, index * lanes : (index + 1) * lanes
-            ]
+        along = turn % groups * (many * chains)
+        base = turn // groups * band_pitch + along
+        for chain in range(chains):
+            spots = [chain * many + index for index in range(many)]
+            field = jnp.concatenate(
+                [grid_ref[pl.ds(base + spot, size, stride=pitch), :] for spot in spots], axis=1
+            )
+            field = apply_left(field)
+            weight = jnp.concatenate(
+                [
+                    potential_ref[pl.ds(pl.multiple_of((along + spot) * size, size), size), :]
+                    for spot in spots
+                ],
+                axis=1,
+            )
+            field = apply_left(field * weight)
+            for index, spot in enumerate(spots):
+                grid_ref[pl.ds(base + spot, size, stride=pitch), :] = field[
+                    :, index * lanes : (index + 1) * lanes
+                ]
         return carry
 
-    turns = pairs * (size // many)
+    turns = pairs * groups
     lax.fori_loop(0, turns, planes, 0)
     lax.fori_loop(0, turns, columns, 0)
     lax.fori_loop(0, turns, planes, 0)
 
-    def collect(block, carry):
+    visits = 12
+
+    def visit(row, wanted, index, value):
+        source = row + lax.shift_right_logical(row, shift) * extra
+        here = lane_gather(grid_ref[pl.ds(source, pairs, stride=band_pitch), :], index)
+        return jnp.where(wanted == row, here, value)
+
+    def slots(block):
         wanted = jnp.broadcast_to(slot_row_ref[pl.ds(block, 1), :], (pairs, lanes))
         index = jnp.broadcast_to(slot_y_ref[pl.ds(block, 1), :], (pairs, lanes))
-        first = first_ref[block]
-        trips = (last_ref[block] - first) // many + 1
-
-        def some(trip, value):
-            for step in range(many):
-                row = jnp.minimum(first + trip * many + step, rows - 1)
-                source = (row // size) * pitch + row % size
-                here = lane_gather(grid_ref[pl.ds(source, pairs, stride=band_pitch), :], index)
-                value = jnp.where(wanted == row, here, value)
-            return value
-
-        out_ref[block] = lax.fori_loop(0, trips, some, jnp.zeros((pairs, lanes), jnp.float32))
+        return wanted, index
+
+    together = math.gcd(blocks, 8)
+
+    def collect(group, carry):
+        longest = 0
+        for step in range(together):
+            block = group * together + step
+            wanted, index = slots(block)
+            first = first_ref[block]
+            value = jnp.zeros((pairs, lanes), jnp.float32)
+            for number in range(visits):
+                value = visit(first + number, wanted, index, value)
+            out_ref[block] = value
+            longest = jnp.maximum(longest, last_ref[block] - first)
+
+        @pl.when(longest >= visits)
+        def _():
+            for step in range(together):
+                block = group * together + step
+                wanted, index = slots(block)
+                first = first_ref[block]
+                out_ref[block] = lax.fori_loop(
+                    first + visits,
+                    last_ref[block] + 1,
+                    lambda row, value: visit(row, wanted, index, value),
+                    out_ref[block],
+                )
+
         return carry
 
-    lax.fori_loop(0, blocks, collect, 0)
-
-
-def grid_call(starts, first, last, code, slot_row, slot_y, potential, left, right, compact, size):
-    blocks, pairs, lanes = compact.shape
+    lax.fori_loop(0, blocks // together, collect, 0)
+
+
+def grid_call(block_of, first, last, code, slot_row, slot_y, potential, left, right, compact, size):
+    _, pairs, lanes = compact.shape
+    blocks = first.shape[0]
     pitch = size + 8
     band_pitch = size * pitch + 8
     smem = pl.BlockSpec(memory_space=pltpu.SMEM)
@@ -474,24 +491,47 @@
         functools.partial(grid_kernel, size=size, pitch=pitch, band_pitch=band_pitch),
         in_specs=[smem] * 3 + [vmem] * 7,
         out_specs=vmem,
-        out_shape=jax.ShapeDtypeStruct(compact.shape, jnp.float32),
-        scratch_shapes=[pltpu.VMEM((pairs * band_pitch, lanes), jnp.float32)],
+        out_shape=jax.ShapeDtypeStruct((blocks, pairs, lanes), jnp.float32),
+        scratch_shapes=[pltpu.VMEM((pairs * band_pitch + 16, lanes), jnp.float32)],
         compiler_params=params(),
         cost_estimate=pl.CostEstimate(
             flops=36 * size * points, bytes_accessed=4 * points, transcendentals=0
         ),
         name="grid",
-    )(starts, first, last, code, slot_row, slot_y, potential, left, right, compact)
-
-
-def finish_kernel(muffin_ref, rest_ref, all_ref, out_ref, sub_ref):
-    bands = out_ref.shape[1]
-
-    @pl.when(pl.program_id(0) == 0)
+    )(block_of, first, last, code, slot_row, slot_y, potential, left, right, compact)
+
+
+def finish_kernel(rank_ref, back_ref, muffin_ref, all_ref, out_ref, sub_ref, rows_ref):
+    block, bands = out_ref.shape
+    parts, _, _, lanes = back_ref.shape
+    half = lanes // 2
+    turn = pl.program_id(0)
+
+    @pl.when(turn == 0)
     def _():
         sub_ref[...] = jnp.zeros_like(sub_ref)
 
-    applied = muffin_ref[...] + rest_ref[...].T
+        def order(tile, carry):
+            start = pl.multiple_of(tile * lanes, lanes)
+            pieces = []
+            for part in range(parts):
+                even = back_ref[part, 2 * tile]
+                odd = back_ref[part, 2 * tile + 1]
+                pieces.append(jnp.concatenate([even[:, :half], odd[:, :half]], axis=1))
+                pieces.append(jnp.concatenate([even[:, half:], odd[:, half:]], axis=1))
+            rows_ref[pl.ds(start, lanes), :] = jnp.concatenate(pieces, axis=0).T
+            return carry
+
+        lax.fori_loop(0, rows_ref.shape[0] // lanes, order, 0)
+
+    first = turn * block
+
+    def place(index, carry):
+        out_ref[pl.ds(index, 1), :] = rows_ref[pl.ds(rank_ref[first + index], 1), :]
+        return carry
+
+    lax.fori_loop(0, block, place, 0, unroll=32)
+    applied = muffin_ref[...] + out_ref[...].T
     out_ref[...] = applied.T
     high, low = split_bf16(applied)
     all_high, all_low = split_bf16(all_ref[...])
@@ -499,16 +539,17 @@
     sub_ref[...] += main[:bands, :] + main[bands:, :] + dot32(high, all_low)
 
 
-def finish_call(muffin, rest, columns):
-    waves, bands = rest.shape
+def finish_call(rank, back, muffin, columns):
+    bands, waves = muffin.shape
     total = columns.shape[1]
     block = math.gcd(waves, 512)
     return pl.pallas_call(
         finish_kernel,
         grid=(waves // block,),
         in_specs=[
+            pl.BlockSpec(memory_space=pltpu.SMEM),
+            pl.BlockSpec(back.shape, lambda i: (0, 0, 0, 0)),
             pl.BlockSpec((bands, block), lambda i: (0, i)),
-            pl.BlockSpec((block, bands), lambda i: (i, 0)),
             pl.BlockSpec((block, total), lambda i: (i, 0)),
         ],
         out_specs=[
@@ -519,9 +560,10 @@
             jax.ShapeDtypeStruct((waves, bands), jnp.float32),
             jax.ShapeDtypeStruct((bands, total), jnp.float32),
         ],
+        scratch_shapes=[pltpu.VMEM((waves, bands), jnp.float32)],
         compiler_params=params("arbitrary"),
         name="finish",
-    )(muffin, rest, columns)
+    )(rank, back, muffin, columns)
 
 
 def exchange(array):
@@ -556,7 +598,7 @@
     return left.astype(jnp.bfloat16), right.astype(jnp.bfloat16)
 
 
-def per_device(wave_coeffs, miller, atom_types, positions, sphere_radii, h_blocks, potential):
+def whole_step(wave_coeffs, miller, atom_types, positions, sphere_radii, h_blocks, potential):
     pw_count = lax.axis_size("pw")
     pw_index = lax.axis_index("pw")
     local_waves, local_bands = wave_coeffs.shape
@@ -573,64 +615,71 @@
     line = (wrapped[2] - pw_index * planes_each) * size + wrapped[0]
     key = line * size + wrapped[1]
     rank = jnp.sum((key[:, None] < key[None, :]).astype(jnp.int32), axis=0)
-    starts = jnp.sum(
-        (line[:, None] < jnp.arange(lines, dtype=jnp.int32)[None, :]).astype(jnp.int32), axis=0
-    )
-    line_onehot = (line[None, :] == jnp.arange(lines, dtype=jnp.int32)[:, None]).astype(
-        jnp.bfloat16
-    )
-    across = jnp.arange(size, dtype=jnp.int32)
-    y_onehot = (wrapped[1][:, None] == across[None, :]).astype(jnp.bfloat16)
-    filled = jnp.dot(line_onehot, y_onehot, preferred_element_type=jnp.float32)
-    before = (across[:, None] < across[None, :]).astype(jnp.bfloat16)
-    ahead = jnp.dot(filled.astype(jnp.bfloat16), before, preferred_element_type=jnp.float32)
-    code = jnp.where(filled > 0.5, ahead, -1024.0)
-
-    send, sorted_key = sort_call(rank, key, wave_coeffs, pw_count, size)
     turned = jnp.transpose(potential, (0, 2, 1))
     pieces = [
         turned.reshape(-1),
-        code.reshape(-1),
-        starts.astype(jnp.float32),
-        sorted_key.astype(jnp.float32),
+        line.astype(jnp.float32),
+        wrapped[1].astype(jnp.float32),
     ]
     cuts = np.cumsum([piece.shape[0] for piece in pieces])
     known = lax.all_gather(jnp.concatenate(pieces), "pw", axis=0, tiled=False)
+
+    send, sorted_key = sort_call(rank, key, wave_coeffs, pw_count, size)
+    blocks_each, pairs, lanes = send.shape[1:]
+    keys = sorted_key.astype(jnp.float32).reshape(1, -1, pairs, lanes)
+    send = jnp.concatenate([send, jnp.broadcast_to(keys, (pw_count,) + keys.shape[1:])], axis=1)
     compact = exchange(send)
 
     spheres, matching_table, phase = sphere_call(
         atom_types, miller, positions, sphere_radii, wave_coeffs, kinds, funcs_each, 2.0 / size
     )
-    atoms_each = atom_total // pw_count
-    parts = exchange(spheres.reshape(pw_count, atoms_each * funcs_each, local_bands))
-    mine = jnp.sum(parts, axis=0).reshape(atoms_each, funcs_each, local_bands)
-    own_types = lax.dynamic_slice_in_dim(atom_types, pw_index * atoms_each, atoms_each, 0)
-    own_onehot = (own_types[:, None] == jnp.arange(kinds, dtype=jnp.int32)[None, :]).astype(
+    spheres = lax.psum(spheres, "pw").reshape(atom_total, funcs_each, local_bands)
+    onehot = (atom_types[:, None] == jnp.arange(kinds, dtype=jnp.int32)[None, :]).astype(
         jnp.float32
     )
-    chosen = jnp.einsum("at,tfk->afk", own_onehot, h_blocks, precision=PRECISE)
-    applied = jnp.einsum("akb,afk->baf", mine, chosen, precision=PRECISE).reshape(
-        1, local_bands, atoms_each * funcs_each
-    )
-    applied = exchange(jnp.broadcast_to(applied, (pw_count,) + applied.shape[1:]))
-    applied = jnp.transpose(applied, (1, 0, 2)).reshape(local_bands, atom_total * funcs_each)
+    chosen = jnp.einsum("at,tfk->afk", onehot, h_blocks, precision=PRECISE)
 
     wave_again, known = lax.optimization_barrier((wave_coeffs, known))
     columns = lax.all_gather(wave_again, "band", axis=1, tiled=True)
 
     field = known[:, : cuts[0]].reshape(size * size, size)
     field = jnp.concatenate([field, field], axis=1)
-    codes = known[:, cuts[0] : cuts[1]].reshape(size * size, size).astype(jnp.int32)
+    all_lines = known[:, cuts[0] : cuts[1]].astype(jnp.int32)
+    all_across = known[:, cuts[1] : cuts[2]].astype(jnp.int32)
+    line_ids = jnp.arange(lines, dtype=jnp.int32)
+    across = jnp.arange(size, dtype=jnp.int32)
+    filled = jnp.einsum(
+        "plg,pgy->ply",
+        (all_lines[:, None, :] == line_ids[None, :, None]).astype(jnp.bfloat16),
+        (all_across[:, :, None] == across[None, None, :]).astype(jnp.bfloat16),
+        preferred_element_type=jnp.float32,
+    )
+    before = (across[:, None] < across[None, :]).astype(jnp.bfloat16)
+    ahead = jnp.einsum(
+        "ply,yv->plv", filled.astype(jnp.bfloat16), before, preferred_element_type=jnp.float32
+    )
+    earlier = (line_ids[:, None] < line_ids[None, :]).astype(jnp.bfloat16)
+    starts = jnp.einsum(
+        "pl,lm->pm",
+        jnp.sum(filled, axis=2).astype(jnp.bfloat16),
+        earlier,
+        preferred_element_type=jnp.float32,
+    ).astype(jnp.int32)
+    starts = starts + jnp.arange(pw_count, dtype=jnp.int32)[:, None] * local_waves
+    block_of = jnp.minimum(starts // size, pw_count * blocks_each - 2)
+    codes = ahead.astype(jnp.int32) + (starts - block_of * size)[:, :, None]
+    codes = jnp.where(filled > 0.5, codes, -1).reshape(size * size, size)
     codes = jnp.concatenate([codes, codes], axis=1)
-    offsets = jnp.arange(pw_count, dtype=jnp.int32)[:, None]
-    all_starts = known[:, cuts[1] : cuts[2]].astype(jnp.int32) + offsets * local_waves
-    all_keys = known[:, cuts[2] : cuts[3]].astype(jnp.int32)
-    all_keys = (all_keys + offsets * (lines * size)).reshape(-1, size)
+
+    all_keys = compact[:, blocks_each:].astype(jnp.int32).reshape(pw_count, -1)
+    offsets = jnp.arange(pw_count, dtype=jnp.int32)[:, None] * (lines * size)
+    all_keys = (all_keys + offsets).reshape(-1, size)
     slot_row = all_keys // size
     slot_y = all_keys % size
+    compact = compact[:, :blocks_each].reshape(-1, pairs, lanes)
     left, right = interstitial_tables(size)
     back = grid_call(
-        all_starts.reshape(-1),
+        block_of.reshape(-1),
         slot_row[:, 0],
         slot_row[:, -1],
         codes,
@@ -639,13 +688,15 @@
         field,
         left,
         right,
-        compact.reshape(-1, *compact.shape[2:]),
+        compact,
         size,
     )
-    back = exchange(back.reshape(compact.shape))
-    muffin = muffin_call(atom_types, matching_table, phase, applied)
-    rest = unsort_call(rank, back, wave_coeffs, kinetic)
-    h_applied, partial = finish_call(muffin, rest, columns)
+    back = exchange(back.reshape(pw_count, blocks_each, pairs, lanes))
+    applied = jnp.einsum("akb,afk->baf", spheres, chosen, precision=PRECISE)
+    muffin = muffin_call(
+        atom_types, matching_table, phase, applied.reshape(local_bands, -1), kinetic, wave_coeffs
+    )
+    h_applied, partial = finish_call(rank, back, muffin, columns)
     partial = jnp.transpose(partial) * factor
     rows_each = partial.shape[0] // pw_count
     gathered = exchange(partial.reshape(pw_count, rows_each, local_bands))
@@ -656,5 +707,5 @@
     in_specs = (P("pw", "band"), P(None, "pw"), P(), P(), P(), P(), P("pw", None, None))
     out_specs = (P("pw", "band"), P("pw", "band"))
     return jax.shard_map(
-        per_device, mesh=mesh, in_specs=in_specs, out_specs=out_specs, check_vma=False
-    )
+        whole_step, mesh=mesh, in_specs=in_specs, out_specs=out_specs, check_vma=False
+    )

time: 512 us -> 334 us (0.65)
  Pallas kernels: 321 us -> 170 us
  waiting for transfers between devices: 100 us -> 62.8 us
  matrix products: 2.82 us -> 19.3 us
  starting transfers between devices: 21.5 us -> 7.87 us
    pallas_call x1, Pallas kernels: 236 us -> 93.4 us  [grid_call(): pl.pallas_call(functools.partial(grid_kernel, size=size, pitch=pitch, ban...]
    all_to_all x4 -> x2, waiting for transfers between devices: 100 us -> 46.6 us  [exchange(): return lax.all_to_all(array, 'pw', split_axis=0, concat_axis=0, tiled=True)]
    dot_general x4 -> x5, matrix products: 2.82 us -> 19.3 us  [the longest x1 13.2 us: whole_step(): jnp.einsum('plg,pgy->ply', (all_lines[:, None, :] == line_ids[None, :, No...]
    all_gather x2, waiting for transfers between devices: 0.01 us -> 16.1 us  [the longest x1 16.1 us: whole_step(): known = lax.all_gather(jnp.concatenate(pieces), 'pw', axis=0, tiled=False)]
    pallas_call x1 -> x0, Pallas kernels: 15.5 us -> none  [unsort_call(): pl.pallas_call(unsort_kernel, in_specs=[pl.BlockSpec(memory_space=pltpu.S...]
    all_to_all x4 -> x2, starting transfers between devices: 21.4 us -> 7.75 us  [exchange(): return lax.all_to_all(array, 'pw', split_axis=0, concat_axis=0, tiled=True)]
    pallas_call x1, Pallas kernels: 8.94 us -> 17.5 us  [finish_call(): pl.pallas_call(finish_kernel, grid=(waves // block,), in_specs=[pl.BlockS...]
    concatenate x4 -> x5, other arithmetic: 4.89 us -> 11.1 us  [the longest x1 4.32 us: whole_step(): codes = jnp.concatenate([codes, codes], axis=1)]
  transfers between devices with their start and end apart: 6 -> 5, of which waited for: 3 -> 3; matrix products, arithmetic and copies ran while one was open for 5% -> 18% of each run, Pallas kernels for 58% -> 46%
where the time goes in v2:
time: 334 us; the launch traced here: 333 us
  Pallas kernels  170 us (51%)
  waiting for transfers between devices  62.8 us (19%)
  other arithmetic  26.5 us (8%)
  local copies, waits for them, and re-layouts  19.9 us (6%)
  matrix products  19.3 us (6%)
  between operations  14 us (4%)
  blocking collectives  12.4 us (4%)
  starting transfers between devices  7.87 us (2%)
    pallas_call x1, Pallas kernels, grid_call(): pl.pallas_call(functools.partial(grid_kernel, size=size, pitch=pitch, ban...  93.4 us
    all_to_all x2, waiting for transfers between devices, exchange(): return lax.all_to_all(array, 'pw', split_axis=0, concat_axis=0, tiled=True)  46.6 us
    pallas_call x1, Pallas kernels, sphere_call(): pl.pallas_call(functools.partial(sphere_kernel, spacing=spacing), grid=(w...  26.2 us
    pallas_call x1, Pallas kernels, muffin_call(): pl.pallas_call(muffin_kernel, grid=(waves // block,), in_specs=[pl.BlockS...  17.9 us
    pallas_call x1, Pallas kernels, finish_call(): pl.pallas_call(finish_kernel, grid=(waves // block,), in_specs=[pl.BlockS...  17.5 us
    all_gather x1, waiting for transfers between devices, whole_step(): known = lax.all_gather(jnp.concatenate(pieces), 'pw', axis=0, tiled=False)  16.1 us
    pallas_call x1, Pallas kernels, sort_call(): pl.pallas_call(sort_kernel, in_specs=[pl.BlockSpec(memory_space=pltpu.SME...  15.4 us
    dot_general x1, matrix products, whole_step(): jnp.einsum('plg,pgy->ply', (all_lines[:, None, :] == line_ids[None, :, No...  13.2 us
  transfers between devices with their start and end apart: 5, of which 3 were waited for; matrix products, arithmetic and copies ran while one was open for 18% of the time, Pallas kernels for 46%

profile of v2, /device:TPU:0, one launch (start us, length us, event | category | flops | bytes accessed | tf_op | source)
XLA Modules:
  0.0 333.1 jit_solution(8543601853892307532)
XLA Ops:
  7.2 0.9 add_select_fusion.2
  8.3 1.1 copy.27
  9.4 0.7 pad_maximum_fusion.2
  10.2 1.4 copy.29
  11.6 1.3 copy.30.radii_ref
  12.9 26.2 %sphere.1 = (f32[2048,128]{1,0:T(8,128)}, f32[4,64,4096]{2,1,0:T(8,128)}, f32[32,4096]{1,0:T(8,128)}) custom-call(s32[32]{0:T(128)} %types_ref.3, s32[3,4096]{1,0:T(4,128)} %miller_ref.1, f32[32,3]{1,0:T(8,128)} %bitcast.43, f32[4,1]{1,0:T(4,128)} %copy.30.radii_ref, f32[4096,128]{1,0:T(8,128)} %wave_ref.5), custom_call_target="tpu_custom_call" | custom-call | flops 6442450944 | bytes 4194304 | tf_op jit(solution)/shard_map/sphere/pallas_call | solution.py:180
  39.2 16.1 %all-gather.6.cloned.1.call-done = f32[327680]{0:T(1024)} async-done(((f32[40960]{0:T(1024)}), f32[327680]{0:T(1024)}) %all-gather.6.cloned.1.call-update) | async-done | bytes 1310736 | tf_op jit(solution)/shard_map/all_gather | solution.py:625
  55.3 2.7 reshape.99
  58.0 8.9 %convert_reduce_fusion.rank_ref = s32[4096]{0:T(1024)} fusion(s32[4096]{0:T(1024)S(1)} %bitcast.39), kind=kLoop, calls=%fused_computation.1 | loop fusion | flops 50327552 | bytes 32768 | tf_op jit(solution)/shard_map/reduce_sum | solution.py:617
  66.9 15.4 %sort.1 = (f32[8,64,8,128]{3,2,1,0:T(8,128)}, s32[4096]{0:T(1024)}) custom-call(s32[4096]{0:T(1024)} %convert_reduce_fusion.rank_ref, s32[4096]{0:T(1024)} %bitcast.40, f32[4096,128]{1,0:T(8,128)} %wave_ref.5), custom_call_target="tpu_custom_call" | custom-call | tf_op jit(solution)/shard_map/sort/pallas_call | solution.py:293
  82.3 0.7 convert_bitcast_fusion
  83.1 3.2 pad_maximum_fusion
  86.3 3.8 %all-to-all-start = ((f32[8,68,8,128]{3,2,1,0:T(8,128)}), f32[8,68,8,128]{3,2,1,0:T(8,128)S(1)}, u32[]{:S(2)}, u32[]{:S(2)}) async-start(f32[8,68,8,128]{3,2,1,0:T(8,128)} %pad_maximum_fusion), calls=%async_computation | async-start | bytes 4456448 | tf_op jit(solution)/shard_map/all_to_all | solution.py:570
  90.1 0.2 subtract_reduce-precision_fusion
  90.3 0.2 fusion.35
  90.4 0.2 fusion.34
  90.6 0.2 fusion.37
  90.8 0.7 pad_maximum_fusion.3.left_ref
  91.7 0.7 fusion.18.right_ref
  92.4 0.7 copy-done.3
  93.1 13.2 %fusion.44 = (bf16[8,512]{1,0:T(8,128)(2,1)S(1)}, f32[8,512,64]{1,2,0:T(8,128)S(1)}) fusion(s32[8,4096]{1,0:T(8,128)S(1)} %get-tuple-element.26, s32[8,4096]{1,0:T(8,128)S(1)} %get-tuple-element.27), kind=kOutput, calls=%fused_computation.102 | convolution fusion | flops 2166616064 | bytes 1318912 | tf_op jit(solution)/shard_map/plg,pgy->ply/dot_general | solution.py:651
  106.3 0.2 multiply_subtract_fusion
  106.5 0.6 copy.35
  107.1 1.3 fusion.4
  108.4 3.2 copy.28
  111.7 2.1 reshape.91
  113.8 4.3 %pad_add_fusion.code_ref = s32[4096,128]{1,0:T(8,128)} fusion(s32[4096,64]{1,0:T(8,128)} %bitcast.32), kind=kLoop, calls=%fused_computation.7 | loop fusion | flops 524288 | bytes 3145728 | tf_op jit(solution)/shard_map/concatenate | solution.py:672
  118.1 1.9 pad_maximum_fusion.1.potential_ref
  120.1 24.1 %all-to-all-done = f32[8,68,8,128]{3,2,1,0:T(8,128)S(1)} async-done(((f32[8,68,8,128]{3,2,1,0:T(8,128)}), f32[8,68,8,128]{3,2,1,0:T(8,128)S(1)}, u32[]{:S(2)}, u32[]{:S(2)}) %all-to-all-start) | async-done | bytes 2228256 | tf_op jit(solution)/shard_map/all_to_all | solution.py:570
  144.2 0.1 reshape.89
  144.3 1.5 slice.47
  145.8 0.3 broadcast_add_fusion
  146.1 0.9 slice_reduce_fusion
  147.0 1.0 pad_add_fusion.1
  148.0 93.4 %grid.1 = f32[512,8,128]{2,1,0:T(8,128)} custom-call(s32[4096]{0:T(1024)} %bitcast.44, s32[512]{0:T(512)} %get-tuple-element.21.first_ref, s32[512]{0:T(512)} %get-tuple-element.20.last_ref, s32[4096,128]{1,0:T(8,128)} %pad_add_fusion.code_ref, s32[512,128]{1,0:T(8,128)} %get-tuple-element.35.slot_row_ref, s32[512,128]{1,0:T(8,128)} %get-tuple-element.36.slot_y_ref, ...), custom_call_target="tpu_custom_call" | custom-call | flops 9663676416 | bytes 16777216 | tf_op jit(solution)/shard_map/grid/pallas_call | solution.py:490
  241.4 4.0 %all-to-all-start.1 = ((f32[8,64,8,128]{3,2,1,0:T(8,128)}), f32[8,64,8,128]{3,2,1,0:T(8,128)S(1)}, u32[]{:S(2)}, u32[]{:S(2)}) async-start(f32[8,64,8,128]{3,2,1,0:T(8,128)} %bitcast.34), calls=%async_computation.1 | async-start | bytes 4194304 | tf_op jit(solution)/shard_map/all_to_all | solution.py:570
  245.5 0.6 broadcast_multiply_fusion
  246.1 0.6 fusion.19
  246.7 3.9 %fusion.6 = f32[32,64,128]{2,1,0:T(8,128)} fusion(f32[32,64,128]{2,1,0:T(8,128)} %all-reduce.7.cloned.1.call-done, f32[32,64,64]{2,0,1:T(8,128)S(1)} %fusion.19), kind=kOutput, calls=%fused_computation.14 | convolution fusion | flops 201326592 | bytes 2621440 | tf_op jit(solution)/shard_map/akb,afk->baf/dot_general | solution.py:695
  250.7 2.6 copy.33.sphere_ref
  253.2 17.9 %muffin.1.muffin_ref = f32[128,4096]{1,0:T(8,128)} custom-call(s32[32]{0:T(128)} %types_ref.3, f32[4,64,4096]{2,1,0:T(8,128)} %get-tuple-element.14.table_ref, f32[32,4096]{1,0:T(8,128)} %get-tuple-element.15.phase_ref, f32[128,2048]{1,0:T(8,128)} %copy.33.sphere_ref, f32[1,4096]{1,0:T(1,128)} %bitcast.45, f32[4096,128]{1,0:T(8,128)} %wave_ref.5), custom_call_target="tpu_custom_call" | custom-call | flops 6442450944 | bytes 4194304 | tf_op jit(solution)/shard_map/muffin/pallas_call | solution.py:238
  271.1 22.5 %all-to-all-done.1.back_ref = f32[8,64,8,128]{3,2,1,0:T(8,128)S(1)} async-done(((f32[8,64,8,128]{3,2,1,0:T(8,128)}), f32[8,64,8,128]{3,2,1,0:T(8,128)S(1)}, u32[]{:S(2)}, u32[]{:S(2)}) %all-to-all-start.1) | async-done | bytes 2097184 | tf_op jit(solution)/shard_map/all_to_all | solution.py:570
  293.6 1.3 copy-done.2
  294.9 17.5 %finish.1 = (f32[4096,128]{1,0:T(8,128)}, f32[128,512]{1,0:T(8,128)}) custom-call(s32[4096]{0:T(1024)} %convert_reduce_fusion.rank_ref, f32[8,64,8,128]{3,2,1,0:T(8,128)} %copy-done.2, f32[128,4096]{1,0:T(8,128)} %muffin.1.muffin_ref, f32[4096,512]{1,0:T(8,128)} %all-gather.4.cloned.1.call-done.all_ref), custom_call_target="tpu_custom_call" | custom-call | tf_op jit(solution)/shard_map/finish/pallas_call | solution.py:546
  312.4 1.0 multiply_bitcast_fusion
  313.4 0.1 copy.34
  313.5 12.4 %all_to_all.15 = f32[8,64,128]{2,1,0:T(8,128)S(1)} all-to-all(f32[8,64,128]{2,1,0:T(8,128)S(1)} %bitcast.37), channel_id=1, replica_groups=mesh['band'=4,'pw'=8] {'pw'}, dimensions={0} | all-to-all | bytes 524288 | tf_op jit(solution)/shard_map/all_to_all | solution.py:570
  325.9 0.6 reduce_sum.39
  (35 shorter events, 0.7 us)
Async XLA Ops:
  7.2 238.9 %copy-start = (f32[4,64,64]{2,1,0:T(8,128)S(1)}, f32[4,64,64]{2,1,0:T(8,128)}, u32[]{:S(2)}) copy-start(f32[4,64,64]{2,1,0:T(8,128)} %param.12) | copy-start | bytes 196612
  7.2 48.1 %all-gather.6.cloned.1.call-start = ((), (), s32[]{:S(2)}) async-start(), calls=%async_computation.5 | async-start | bytes 1474560 | tf_op jit(solution)/shard_map/all_gather | solution.py:625
  8.2 49.8 %copy-start.5 = (s32[1,4096]{1,0:T(1,128)}, s32[1,4096]{1,0:T(1,128)S(1)}, u32[]{:S(2)}) copy-start(s32[1,4096]{1,0:T(1,128)S(1)} %get-tuple-element.30) | copy-start | bytes 49156
  10.1 236.6 %all-reduce.7.cloned.1.call-start = ((), (), s32[]{:S(2)}) async-start(), calls=%async_computation.3 | async-start | bytes 2097152 | tf_op jit(solution)/shard_map/psum | solution.py:636
  39.2 254.5 %all-gather.4.cloned.1.call-start = ((), (), s32[]{:S(2)}) async-start(), calls=%async_computation.4 | async-start | bytes 10485760 | tf_op jit(solution)/shard_map/all_gather | solution.py:643
  86.3 57.9 %all-to-all-start = ((f32[8,68,8,128]{3,2,1,0:T(8,128)}), f32[8,68,8,128]{3,2,1,0:T(8,128)S(1)}, u32[]{:S(2)}, u32[]{:S(2)}) async-start(f32[8,68,8,128]{3,2,1,0:T(8,128)} %pad_maximum_fusion), calls=%async_computation | async-start | bytes 4456448 | tf_op jit(solution)/shard_map/all_to_all | solution.py:570
  91.7 1.4 copy-start.3
  108.4 3.2 slice-start
  113.8 4.3 %copy-start.1 = (f32[4096,64]{1,0:T(8,128)S(1)}, f32[4096,64]{1,0:T(8,128)}, u32[]{:S(2)}) copy-start(f32[4096,64]{1,0:T(8,128)} %reshape.91) | copy-start | bytes 3145732
  241.4 4.0 %copy-start.4 = (s32[3,4096]{1,0:T(4,128)S(1)}, s32[3,4096]{1,0:T(4,128)}, u32[]{:S(2)}) copy-start(s32[3,4096]{1,0:T(4,128)} %miller_ref.1) | copy-start | bytes 147460
  241.4 4.6 %copy-start.6 = (s32[32]{0:T(128)S(1)}, s32[32]{0:T(128)}, u32[]{:S(2)}) copy-start(s32[32]{0:T(128)} %types_ref.3) | copy-start | bytes 388
  241.4 52.2 %all-to-all-start.1 = ((f32[8,64,8,128]{3,2,1,0:T(8,128)}), f32[8,64,8,128]{3,2,1,0:T(8,128)S(1)}, u32[]{:S(2)}, u32[]{:S(2)}) async-start(f32[8,64,8,128]{3,2,1,0:T(8,128)} %bitcast.34), calls=%async_computation.1 | async-start | bytes 4194304 | tf_op jit(solution)/shard_map/all_to_all | solution.py:570
  293.6 1.3 copy-start.2
Sparse Core Ops, SparseCore 0:
  10.7 44.5 all-gather.5
  58.8 98.3 all-reduce.6
  158.8 58.9 all-gather.3

commit v3 on v2

--- a/solution.py
+++ b/solution.py
@@ -175,7 +175,7 @@
 def sphere_call(types, miller, positions, radii, wave, kinds, funcs, spacing):
     waves, bands = wave.shape
     atoms = positions.shape[1]
-    block = math.gcd(waves, 512)
+    block = math.gcd(waves, 1024)
     rows = atoms * funcs
     return pl.pallas_call(
         functools.partial(sphere_kernel, spacing=spacing),
@@ -234,7 +234,7 @@
     kinds, funcs, waves = table.shape
     atoms = phase.shape[0]
     bands, rows = sphere.shape
-    block = math.gcd(waves, 512)
+    block = math.gcd(waves, 1024)
     return pl.pallas_call(
         muffin_kernel,
         grid=(waves // block,),
@@ -290,6 +290,7 @@
 def sort_call(rank, key, wave, parts, half):
     waves, bands = wave.shape
     pairs = bands // parts // 2
+    stored = waves // half + waves // (pairs * 2 * half)
     return pl.pallas_call(
         sort_kernel,
         in_specs=[
@@ -302,7 +303,7 @@
             pl.BlockSpec(memory_space=pltpu.SMEM),
         ],
         out_shape=[
-            jax.ShapeDtypeStruct((parts, waves // half, pairs, 2 * half), jnp.float32),
+            jax.ShapeDtypeStruct((parts, stored, pairs, 2 * half), jnp.float32),
             jax.ShapeDtypeStruct((waves,), jnp.int32),
         ],
         scratch_shapes=[pltpu.VMEM((waves, bands), jnp.float32)],
@@ -329,7 +330,8 @@
 
 
 def grid_kernel(
-    block_ref,
+    window_ref,
+    deep_ref,
     first_ref,
     last_ref,
     code_ref,
@@ -341,10 +343,12 @@
     compact_ref,
     out_ref,
     grid_ref,
+    windows_ref,
     *,
     size,
     pitch,
     band_pitch,
+    wide,
 ):
     blocks, pairs, lanes = out_ref.shape
     half = lanes // 2
@@ -352,21 +356,70 @@
     shift = size.bit_length() - 1
     extra = pitch - size
     upper = lax.broadcasted_iota(jnp.int32, (pairs, lanes), 1) // half * half
-    wide = math.gcd(rows, 64)
+    parts, _, _, _ = compact_ref.shape
+    each = blocks // parts
+    inner = lax.broadcasted_iota(jnp.int32, (pairs, lanes), 1) % half
+    steps = math.gcd(each, 16)
+
+    def widen(part, carry):
+        following = jnp.minimum(part + 1, parts - 1)
+
+        def some(group, carry):
+            first = group * steps
+            for step in range(steps):
+                block = compact_ref[part, first + step]
+                if step + 1 < steps:
+                    after = compact_ref[part, first + step + 1]
+                else:
+                    inside = first + steps < each
+                    after = compact_ref[
+                        jnp.where(inside, part, following), jnp.where(inside, first + steps, 0)
+                    ]
+                mixed = jnp.where(
+                    inner < half // 2,
+                    pltpu.roll(block, lanes - half // 2, 1),
+                    pltpu.roll(after, half // 2, 1),
+                )
+                spot = 2 * (part * each + first + step)
+                windows_ref[spot] = block
+                windows_ref[spot + 1] = mixed
+            return carry
+
+        return lax.fori_loop(0, each // steps, some, carry)
+
+    lax.fori_loop(0, parts, widen, 0)
 
     def expand(group, carry):
         base = group * wide
         place = base + lax.shift_right_logical(base, shift) * extra
-        for step in range(wide):
-            row = base + step
-            block = block_ref[row]
-            code = jnp.broadcast_to(code_ref[pl.ds(row, 1), :], (pairs, lanes))
-            index = (code & (half - 1)) | upper
-            here = lane_gather(compact_ref[block], index)
-            there = lane_gather(compact_ref[block + 1], index)
-            value = jnp.where(code < half, here, there)
-            value = jnp.where(code >= 0, value, 0.0)
-            grid_ref[pl.ds(place + step, pairs, stride=band_pitch), :] = value
+
+        @pl.when(deep_ref[group] == 0)
+        def _():
+            for step in range(wide):
+                row = base + step
+                code = jnp.broadcast_to(code_ref[pl.ds(row, 1), :], (pairs, lanes))
+                index = (code & (half - 1)) | upper
+                value = lane_gather(windows_ref[window_ref[row]], index)
+                value = jnp.where(code >= 0, value, 0.0)
+                grid_ref[pl.ds(place + step, pairs, stride=band_pitch), :] = value
+
+        @pl.when(deep_ref[group] != 0)
+        def _():
+            def one(step, carry):
+                row = base + step
+                code = jnp.broadcast_to(code_ref[pl.ds(row, 1), :], (pairs, lanes))
+                index = (code & (half - 1)) | upper
+                window = window_ref[row]
+                later = jnp.minimum(window + 2, 2 * blocks - 1)
+                here = lane_gather(windows_ref[window], index)
+                there = lane_gather(windows_ref[later], index)
+                value = jnp.where(code < half, here, there)
+                value = jnp.where(code >= 0, value, 0.0)
+                grid_ref[pl.ds(place + step, pairs, stride=band_pitch), :] = value
+                return carry
+
+            lax.fori_loop(0, wide, one, 0)
+
         return carry
 
     lax.fori_loop(0, rows // wide, expand, 0)
@@ -479,8 +532,8 @@
     lax.fori_loop(0, blocks // together, collect, 0)
 
 
-def grid_call(block_of, first, last, code, slot_row, slot_y, potential, left, right, compact, size):
-    _, pairs, lanes = compact.shape
+def grid_call(window, deep, first, last, code, slot_row, slot_y, field, left, right, compact, size):
+    _, _, pairs, lanes = compact.shape
     blocks = first.shape[0]
     pitch = size + 8
     band_pitch = size * pitch + 8
@@ -488,20 +541,120 @@
     vmem = pl.BlockSpec(memory_space=pltpu.VMEM)
     points = 2 * pairs * size**3
     return pl.pallas_call(
-        functools.partial(grid_kernel, size=size, pitch=pitch, band_pitch=band_pitch),
-        in_specs=[smem] * 3 + [vmem] * 7,
+        functools.partial(
+            grid_kernel,
+            size=size,
+            pitch=pitch,
+            band_pitch=band_pitch,
+            wide=size * size // deep.shape[0],
+        ),
+        in_specs=[smem] * 4 + [vmem] * 7,
         out_specs=vmem,
         out_shape=jax.ShapeDtypeStruct((blocks, pairs, lanes), jnp.float32),
-        scratch_shapes=[pltpu.VMEM((pairs * band_pitch + 16, lanes), jnp.float32)],
+        scratch_shapes=[
+            pltpu.VMEM((pairs * band_pitch + 16, lanes), jnp.float32),
+            pltpu.VMEM((2 * blocks, pairs, lanes), jnp.float32),
+        ],
         compiler_params=params(),
         cost_estimate=pl.CostEstimate(
             flops=36 * size * points, bytes_accessed=4 * points, transcendentals=0
         ),
         name="grid",
-    )(block_of, first, last, code, slot_row, slot_y, potential, left, right, compact)
-
-
-def finish_kernel(rank_ref, back_ref, muffin_ref, all_ref, out_ref, sub_ref, rows_ref):
+    )(window, deep, first, last, code, slot_row, slot_y, field, left, right, compact)
+
+
+def prepare_kernel(known_ref, lanes_ref, rows_ref, code_ref, field_ref, *, waves, low_count, size):
+    lanes = known_ref.shape[2]
+    left_ids, right_ids = rows_ref.shape[0], lanes_ref.shape[0]
+    field_rows = code_ref.shape[1] // 2
+    wave_rows = waves // lanes
+    part = pl.program_id(0)
+
+    def onehot(first, count):
+        ids = lax.broadcasted_iota(jnp.int32, (count, lanes), 0).astype(jnp.float32)
+        return jnp.concatenate(
+            [
+                jnp.where(known_ref[0, row : row + 1, :] == ids, 1.0, 0.0).astype(jnp.bfloat16)
+                for row in range(first, first + wave_rows)
+            ],
+            axis=1,
+        )
+
+    filled = lax.dot_general(
+        onehot(field_rows, left_ids),
+        onehot(field_rows + wave_rows, right_ids),
+        (((1,), (1,)), ((), ())),
+        preferred_element_type=jnp.float32,
+    )
+    sums = dot32(filled.astype(jnp.bfloat16), lanes_ref[...])
+    ahead = sums[:, :right_ids]
+    counts = jnp.concatenate(
+        [sums[:, index * right_ids : (index + 1) * right_ids] for index in (1, 2, 3)], axis=0
+    )
+    start = dot32(rows_ref[...], counts.astype(jnp.bfloat16)).astype(jnp.int32) + part * waves
+    code = ahead.astype(jnp.int32) + (start & (size // 2 - 1))
+    code = jnp.where(filled > 0.5, code, -1)
+    for low in range(low_count):
+        piece = code[:, low * size : (low + 1) * size]
+        piece = jnp.concatenate([piece, piece], axis=1)
+        for high in range(left_ids // size):
+            first = (high * low_count + low) * size
+            code_ref[0, first : first + size, :] = piece[high * size : (high + 1) * size, :]
+    field = known_ref[0, :field_rows, :]
+    for side in range(2):
+        half = field[:, side * size : (side + 1) * size]
+        field_ref[0, pl.ds(side, field_rows, stride=2), :] = jnp.concatenate([half, half], axis=1)
+
+
+def prepare_call(known, waves, planes_each, size):
+    parts, stored, lanes = known.shape
+    low_count = math.gcd(planes_each, 4)
+    high_count = planes_each // low_count
+    lines = planes_each * size
+    eye = np.eye(low_count)
+    square = np.ones((size, size))
+    before = np.triu(square, 1)
+    lanes_table = np.concatenate(
+        [
+            np.kron(eye, before),
+            np.kron(eye, square),
+            np.kron(np.triu(np.ones((low_count, low_count)), 1), square),
+            np.kron(np.ones((low_count, low_count)), square),
+        ],
+        axis=1,
+    )
+    eye = np.eye(high_count)
+    rows_table = np.concatenate(
+        [
+            np.kron(eye, before.T),
+            np.kron(eye, square),
+            np.kron(np.tril(np.ones((high_count, high_count)), -1), square),
+        ],
+        axis=1,
+    )
+    return pl.pallas_call(
+        functools.partial(prepare_kernel, waves=waves, low_count=low_count, size=size),
+        grid=(parts,),
+        in_specs=[
+            pl.BlockSpec((1, stored, lanes), lambda i: (i, 0, 0)),
+            pl.BlockSpec(lanes_table.shape, lambda i: (0, 0)),
+            pl.BlockSpec(rows_table.shape, lambda i: (0, 0)),
+        ],
+        out_specs=[pl.BlockSpec((1, lines, lanes), lambda i: (i, 0, 0))] * 2,
+        out_shape=[
+            jax.ShapeDtypeStruct((parts, lines, lanes), jnp.int32),
+            jax.ShapeDtypeStruct((parts, lines, lanes), jnp.float32),
+        ],
+        compiler_params=params("arbitrary"),
+        cost_estimate=pl.CostEstimate(
+            flops=2 * parts * waves * lines * size, bytes_accessed=4 * parts * waves, transcendentals=0
+        ),
+        name="prepare",
+    )(known, jnp.asarray(lanes_table, jnp.bfloat16), jnp.asarray(rows_table, jnp.bfloat16))
+
+
+def finish_kernel(rank_ref, where_ref, back_ref, muffin_ref, *refs):
+    *all_refs, out_ref, sub_ref, rows_ref = refs
     block, bands = out_ref.shape
     parts, _, _, lanes = back_ref.shape
     half = lanes // 2
@@ -522,7 +675,7 @@
             rows_ref[pl.ds(start, lanes), :] = jnp.concatenate(pieces, axis=0).T
             return carry
 
-        lax.fori_loop(0, rows_ref.shape[0] // lanes, order, 0)
+        lax.fori_loop(0, rows_ref.shape[0] // lanes, order, 0, unroll=4)
 
     first = turn * block
 
@@ -530,40 +683,49 @@
         out_ref[pl.ds(index, 1), :] = rows_ref[pl.ds(rank_ref[first + index], 1), :]
         return carry
 
-    lax.fori_loop(0, block, place, 0, unroll=32)
+    lax.fori_loop(0, block, place, 0, unroll=64)
     applied = muffin_ref[...] + out_ref[...].T
     out_ref[...] = applied.T
     high, low = split_bf16(applied)
-    all_high, all_low = split_bf16(all_ref[...])
-    main = dot32(jnp.concatenate([high, low], axis=0), all_high)
-    sub_ref[...] += main[:bands, :] + main[bands:, :] + dot32(high, all_low)
-
-
-def finish_call(rank, back, muffin, columns):
+    both = jnp.concatenate([high, low], axis=0)
+    for shift, all_ref in enumerate(all_refs):
+        all_high, all_low = split_bf16(all_ref[...])
+        main = dot32(both, all_high)
+        total = main[:bands, :] + main[bands:, :] + dot32(high, all_low)
+        sub_ref[where_ref[shift]] += total
+
+    @pl.when(turn == pl.num_programs(0) - 1)
+    def _():
+        for group in range(sub_ref.shape[0]):
+            sub_ref[group] = sub_ref[group].T * NPW ** (-0.5)
+
+
+def finish_call(rank, where, back, muffin, columns):
     bands, waves = muffin.shape
-    total = columns.shape[1]
-    block = math.gcd(waves, 512)
+    groups = len(columns)
+    block = math.gcd(waves, 2048)
     return pl.pallas_call(
         finish_kernel,
         grid=(waves // block,),
         in_specs=[
             pl.BlockSpec(memory_space=pltpu.SMEM),
+            pl.BlockSpec(memory_space=pltpu.SMEM),
             pl.BlockSpec(back.shape, lambda i: (0, 0, 0, 0)),
             pl.BlockSpec((bands, block), lambda i: (0, i)),
-            pl.BlockSpec((block, total), lambda i: (i, 0)),
-        ],
+        ]
+        + [pl.BlockSpec((block, bands), lambda i: (i, 0))] * groups,
         out_specs=[
             pl.BlockSpec((block, bands), lambda i: (i, 0)),
-            pl.BlockSpec((bands, total), lambda i: (0, 0)),
+            pl.BlockSpec((groups, bands, bands), lambda i: (0, 0, 0)),
         ],
         out_shape=[
             jax.ShapeDtypeStruct((waves, bands), jnp.float32),
-            jax.ShapeDtypeStruct((bands, total), jnp.float32),
+            jax.ShapeDtypeStruct((groups, bands, bands), jnp.float32),
         ],
         scratch_shapes=[pltpu.VMEM((waves, bands), jnp.float32)],
         compiler_params=params("arbitrary"),
         name="finish",
-    )(rank, back, muffin, columns)
+    )(rank, where, back, muffin, *columns)
 
 
 def exchange(array):
@@ -605,81 +767,78 @@
     size = potential.shape[1]
     kinds, funcs_each = h_blocks.shape[:2]
     atom_total = atom_types.shape[0]
-    factor = NPW ** (-0.5)
     miller_float = miller.astype(jnp.float32)
     kinetic = jnp.sum(miller_float * miller_float, axis=0) / 1536.0
     planes_each = size // pw_count
     lines = planes_each * size
 
+    group_count = lax.axis_size("band")
+    group = lax.axis_index("band")
+    columns = [wave_coeffs]
+    for shift in range(1, group_count):
+        route = [(index, (index + shift) % group_count) for index in range(group_count)]
+        columns.append(lax.ppermute(wave_coeffs, "band", route))
+    where = jnp.mod(group - jnp.arange(group_count, dtype=jnp.int32), group_count)
+
     wrapped = jnp.mod(miller, size)
     line = (wrapped[2] - pw_index * planes_each) * size + wrapped[0]
     key = line * size + wrapped[1]
     rank = jnp.sum((key[:, None] < key[None, :]).astype(jnp.int32), axis=0)
-    turned = jnp.transpose(potential, (0, 2, 1))
+    lanes = 2 * size
+    low_count = math.gcd(planes_each, 4)
+    plane = wrapped[2] - pw_index * planes_each
+    starts = jnp.sum(
+        (line[:, None] < jnp.arange(lines, dtype=jnp.int32)[None, :]).astype(jnp.int32), axis=0
+    )
     pieces = [
-        turned.reshape(-1),
-        line.astype(jnp.float32),
-        wrapped[1].astype(jnp.float32),
+        jnp.transpose(potential, (0, 2, 1)),
+        (plane // low_count * size + wrapped[0]).astype(jnp.float32),
+        (plane % low_count * size + wrapped[1]).astype(jnp.float32),
+        starts.astype(jnp.float32),
     ]
+    pieces = [piece.reshape(-1, lanes) for piece in pieces]
     cuts = np.cumsum([piece.shape[0] for piece in pieces])
+    pieces.append(jnp.zeros((-int(cuts[-1]) % 8, lanes), jnp.float32))
     known = lax.all_gather(jnp.concatenate(pieces), "pw", axis=0, tiled=False)
 
     send, sorted_key = sort_call(rank, key, wave_coeffs, pw_count, size)
-    blocks_each, pairs, lanes = send.shape[1:]
+    _, pairs = send.shape[1:3]
+    blocks_each = local_waves // size
     keys = sorted_key.astype(jnp.float32).reshape(1, -1, pairs, lanes)
-    send = jnp.concatenate([send, jnp.broadcast_to(keys, (pw_count,) + keys.shape[1:])], axis=1)
+    send = send.at[:, blocks_each:].set(jnp.broadcast_to(keys, (pw_count,) + keys.shape[1:]))
     compact = exchange(send)
 
     spheres, matching_table, phase = sphere_call(
         atom_types, miller, positions, sphere_radii, wave_coeffs, kinds, funcs_each, 2.0 / size
     )
-    spheres = lax.psum(spheres, "pw").reshape(atom_total, funcs_each, local_bands)
     onehot = (atom_types[:, None] == jnp.arange(kinds, dtype=jnp.int32)[None, :]).astype(
         jnp.float32
     )
     chosen = jnp.einsum("at,tfk->afk", onehot, h_blocks, precision=PRECISE)
 
-    wave_again, known = lax.optimization_barrier((wave_coeffs, known))
-    columns = lax.all_gather(wave_again, "band", axis=1, tiled=True)
-
-    field = known[:, : cuts[0]].reshape(size * size, size)
-    field = jnp.concatenate([field, field], axis=1)
-    all_lines = known[:, cuts[0] : cuts[1]].astype(jnp.int32)
-    all_across = known[:, cuts[1] : cuts[2]].astype(jnp.int32)
-    line_ids = jnp.arange(lines, dtype=jnp.int32)
-    across = jnp.arange(size, dtype=jnp.int32)
-    filled = jnp.einsum(
-        "plg,pgy->ply",
-        (all_lines[:, None, :] == line_ids[None, :, None]).astype(jnp.bfloat16),
-        (all_across[:, :, None] == across[None, None, :]).astype(jnp.bfloat16),
-        preferred_element_type=jnp.float32,
-    )
-    before = (across[:, None] < across[None, :]).astype(jnp.bfloat16)
-    ahead = jnp.einsum(
-        "ply,yv->plv", filled.astype(jnp.bfloat16), before, preferred_element_type=jnp.float32
-    )
-    earlier = (line_ids[:, None] < line_ids[None, :]).astype(jnp.bfloat16)
-    starts = jnp.einsum(
-        "pl,lm->pm",
-        jnp.sum(filled, axis=2).astype(jnp.bfloat16),
-        earlier,
-        preferred_element_type=jnp.float32,
-    ).astype(jnp.int32)
-    starts = starts + jnp.arange(pw_count, dtype=jnp.int32)[:, None] * local_waves
-    block_of = jnp.minimum(starts // size, pw_count * blocks_each - 2)
-    codes = ahead.astype(jnp.int32) + (starts - block_of * size)[:, :, None]
-    codes = jnp.where(filled > 0.5, codes, -1).reshape(size * size, size)
-    codes = jnp.concatenate([codes, codes], axis=1)
+    codes, field = prepare_call(known, local_waves, planes_each, size)
+    codes = codes.reshape(size * size, lanes)
+    field = field.reshape(size * size, lanes)
+    offsets = jnp.arange(pw_count, dtype=jnp.int32)[:, None]
+    all_starts = known[:, cuts[2] : cuts[3]].reshape(pw_count, lines).astype(jnp.int32)
+    all_starts = (all_starts + offsets * local_waves).reshape(-1)
+    total = pw_count * local_waves
+    ends = jnp.concatenate([all_starts[1:], jnp.full((1,), total, jnp.int32)])
+    window = jnp.minimum(all_starts // (size // 2), total // (size // 2) - 1)
+    reach = (all_starts % (size // 2)) + (ends - all_starts)
+    deep = jnp.max(reach.reshape(size, size), axis=1) > size
 
     all_keys = compact[:, blocks_each:].astype(jnp.int32).reshape(pw_count, -1)
-    offsets = jnp.arange(pw_count, dtype=jnp.int32)[:, None] * (lines * size)
-    all_keys = (all_keys + offsets).reshape(-1, size)
+    all_keys = (all_keys + offsets * (lines * size)).reshape(-1, size)
     slot_row = all_keys // size
     slot_y = all_keys % size
-    compact = compact[:, :blocks_each].reshape(-1, pairs, lanes)
+    spheres, slot_y = lax.optimization_barrier((spheres, slot_y))
+    spheres = lax.psum(spheres, "pw")
+    spheres = spheres.reshape(atom_total, funcs_each, local_bands)
     left, right = interstitial_tables(size)
     back = grid_call(
-        block_of.reshape(-1),
+        window,
+        deep.astype(jnp.int32),
         slot_row[:, 0],
         slot_row[:, -1],
         codes,
@@ -696,9 +855,8 @@
     muffin = muffin_call(
         atom_types, matching_table, phase, applied.reshape(local_bands, -1), kinetic, wave_coeffs
     )
-    h_applied, partial = finish_call(rank, back, muffin, columns)
-    partial = jnp.transpose(partial) * factor
-    rows_each = partial.shape[0] // pw_count
+    h_applied, partial = finish_call(rank, where, back, muffin, columns)
+    rows_each = group_count * local_bands // pw_count
     gathered = exchange(partial.reshape(pw_count, rows_each, local_bands))
     return (h_applied, jnp.sum(gathered, axis=0))
 

time: 334 us -> 391 us (1.17)
  waiting for transfers between devices: 62.8 us -> 137 us
  matrix products: 19.3 us -> 4.56 us
  local copies, waits for them, and re-layouts: 19.9 us -> 9.01 us
  Pallas kernels: 170 us -> 178 us
  starting transfers between devices: 7.87 us -> 15.1 us
  other arithmetic: 26.5 us -> 19.8 us
    psum x1, waiting for transfers between devices: 0.02 us -> 104 us  [whole_step(): spheres = lax.psum(spheres, 'pw')]
    all_to_all x2, waiting for transfers between devices: 46.6 us -> 0.01 us  [exchange(): return lax.all_to_all(array, 'pw', split_axis=0, concat_axis=0, tiled=True)]
    all_gather x1, waiting for transfers between devices: 16.1 us -> 32.9 us  [whole_step(): known = lax.all_gather(jnp.concatenate(pieces), 'pw', axis=0, tiled=False)]
    dot_general x3 -> x0, matrix products: 14.7 us -> none  [the longest x1 13.2 us: whole_step(): jnp.einsum('plg,pgy->ply', (all_lines[:, None, :] == line_ids[None, :, No...]
    pallas_call x0 -> x1, Pallas kernels: none -> 13.4 us  [prepare_call(): pl.pallas_call(functools.partial(prepare_kernel, waves=waves, low_count=l...]
    concatenate x4 -> x2, other arithmetic: 10.1 us -> 0.91 us  [the longest x1 0.84 us: whole_step(): jnp.concatenate([slot_y, slot_y + size], axis=1)]
    pallas_call x1, Pallas kernels: 93.4 us -> 88.3 us  [grid_call(): pl.pallas_call(functools.partial(grid_kernel, size=size, pitch=pitch, ban...]
    all_to_all x2, starting transfers between devices: 7.75 us -> 12.1 us  [exchange(): return lax.all_to_all(array, 'pw', split_axis=0, concat_axis=0, tiled=True)]
  transfers between devices with their start and end apart: 5 -> 7, of which waited for: 3 -> 2; matrix products, arithmetic and copies ran while one was open for 18% -> 5% of each run, Pallas kernels for 46% -> 15%
where the time goes in v3:
time: 391 us; the launch traced here: 390 us
  Pallas kernels  178 us (46%)
  waiting for transfers between devices  137 us (35%)
  other arithmetic  19.8 us (5%)
  starting transfers between devices  15.1 us (4%)
  between operations  14.3 us (4%)
  blocking collectives  12.6 us (3%)
  local copies, waits for them, and re-layouts  9.01 us (2%)
  matrix products  4.56 us (1%)
    psum x1, waiting for transfers between devices, whole_step(): spheres = lax.psum(spheres, 'pw')  104 us
    pallas_call x1, Pallas kernels, grid_call(): pl.pallas_call(functools.partial(grid_kernel, size=size, pitch=pitch, ban...  88.3 us
    all_gather x1, waiting for transfers between devices, whole_step(): known = lax.all_gather(jnp.concatenate(pieces), 'pw', axis=0, tiled=False)  32.9 us
    pallas_call x1, Pallas kernels, sphere_call(): pl.pallas_call(functools.partial(sphere_kernel, spacing=spacing), grid=(w...  26.6 us
    pallas_call x1, Pallas kernels, muffin_call(): pl.pallas_call(muffin_kernel, grid=(waves // block,), in_specs=[pl.BlockS...  18.5 us
    pallas_call x1, Pallas kernels, finish_call(): pl.pallas_call(finish_kernel, grid=(waves // block,), in_specs=[pl.BlockS...  15.6 us
    pallas_call x1, Pallas kernels, sort_call(): pl.pallas_call(sort_kernel, in_specs=[pl.BlockSpec(memory_space=pltpu.SME...  15.5 us
    pallas_call x1, Pallas kernels, prepare_call(): pl.pallas_call(functools.partial(prepare_kernel, waves=waves, low_count=l...  13.4 us
  transfers between devices with their start and end apart: 7, of which 2 were waited for; matrix products, arithmetic and copies ran while one was open for 5% of the time, Pallas kernels for 15%

profile of v3, /device:TPU:0, one launch (start us, length us, event | category | flops | bytes accessed | tf_op | source)
XLA Modules:
  0.0 390.2 jit_solution(15161176176610575074)
XLA Ops:
  7.2 0.9 add_select_fusion.2
  8.2 8.9 %convert_reduce_fusion.rank_ref = s32[4096]{0:T(1024)} fusion(s32[4096]{0:T(1024)S(1)} %bitcast.48, s32[4096]{0:T(1024)S(1)} %multiply_add_fusion.1.key_ref), kind=kLoop, calls=%fused_computation | loop fusion | flops 50327552 | bytes 49152 | tf_op jit(solution)/shard_map/reduce_sum | solution.py:786
  17.1 15.5 %sort.1 = (f32[8,68,8,128]{3,2,1,0:T(8,128)}, s32[4096]{0:T(1024)}) custom-call(s32[4096]{0:T(1024)} %convert_reduce_fusion.rank_ref, s32[4096]{0:T(1024)} %copy-done.5, f32[4096,128]{1,0:T(8,128)} %refs_0_.1), custom_call_target="tpu_custom_call" | custom-call | tf_op jit(solution)/shard_map/sort/pallas_call | solution.py:294
  32.7 0.7 convert_bitcast_fusion
  33.4 0.7 broadcast_dynamic-update-slice_fusion
  34.1 7.4 %all-to-all-start = ((f32[8,68,8,128]{3,2,1,0:T(8,128)}), f32[8,68,8,128]{3,2,1,0:T(8,128)S(1)}, u32[]{:S(2)}, u32[]{:S(2)}) async-start(f32[8,68,8,128]{3,2,1,0:T(8,128)} %broadcast_dynamic-update-slice_fusion), calls=%async_computation | async-start | bytes 4456448 | tf_op jit(solution)/shard_map/all_to_all | solution.py:732
  41.6 1.0 convert_reduce_fusion.1
  42.5 0.1 copy.18
  42.7 0.1 reshape.137
  42.8 2.5 concatenate.58
  45.4 0.1 add.164
  45.5 0.7 copy.19
  46.2 0.7 copy.20.radii_ref
  47.0 0.1 add.158
  47.1 0.2 subtract_reduce-precision_fusion
  47.3 0.2 fusion.34
  47.4 0.2 fusion.38
  47.6 0.2 fusion.35
  47.8 0.1 fusion.15
  47.8 0.7 pad_maximum_fusion.left_ref
  48.5 0.7 fusion.11.right_ref
  49.3 26.6 %sphere.1 = (f32[2048,128]{1,0:T(8,128)}, f32[4,64,4096]{2,1,0:T(8,128)}, f32[32,4096]{1,0:T(8,128)}) custom-call(s32[32]{0:T(128)} %types_ref.3, s32[3,4096]{1,0:T(4,128)} %miller_ref.1, f32[32,3]{1,0:T(8,128)} %bitcast.46, f32[4,1]{1,0:T(4,128)} %copy.20.radii_ref, f32[4096,128]{1,0:T(8,128)} %refs_0_.1), custom_call_target="tpu_custom_call" | custom-call | flops 6442450944 | bytes 4194304 | tf_op jit(solution)/shard_map/sphere/pallas_call | solution.py:180
  75.9 32.9 %all-gather.3.cloned.1.call-done = f32[2624,128]{1,0:T(8,128)} async-done(((f32[328,128]{1,0:T(8,128)}), f32[2624,128]{1,0:T(8,128)}) %all-gather.3.cloned.1.call-update) | async-done | bytes 1343504 | tf_op jit(solution)/shard_map/all_gather | solution.py:802
  108.8 0.8 slice_convert_fusion.1
  109.6 0.1 convert_element_type.68
  109.7 0.6 fusion.33
  110.5 0.2 fusion.18
  110.7 13.4 %prepare.1 = (s32[8,512,128]{2,1,0:T(8,128)}, f32[8,512,128]{2,1,0:T(8,128)}) custom-call(f32[8,328,128]{2,1,0:T(8,128)} %bitcast.51, bf16[256,1024]{1,0:T(8,128)(2,1)} %constant.167.clone.lanes_ref, bf16[128,384]{1,0:T(8,128)(2,1)} %constant.168.clone.rows_ref), custom_call_target="tpu_custom_call" | custom-call | flops 2147483648 | bytes 131072 | tf_op jit(solution)/shard_map/prepare/pallas_call | solution.py:635
  124.1 0.5 compare_convert_fusion.deep_ref
  124.6 0.1 reshape.138
  124.7 0.3 add_select_fusion
  125.1 0.9 slice_reduce_fusion
  126.0 0.8 pad_add_fusion.slot_row_ref
  126.9 0.8 pad_add_fusion.1.slot_y_ref
  127.7 88.3 %grid.1 = f32[512,8,128]{2,1,0:T(8,128)} custom-call(s32[4096]{0:T(1024)} %get-tuple-element.38.window_ref, s32[64]{0:T(128)} %compare_convert_fusion.deep_ref, s32[512]{0:T(512)} %get-tuple-element.37.first_ref, s32[512]{0:T(512)} %get-tuple-element.36.last_ref, s32[4096,128]{1,0:T(8,128)} %bitcast.52, s32[512,128]{1,0:T(8,128)} %pad_add_fusion.slot_row_ref, ...), custom_call_target="tpu_custom_call" | custom-call | flops 9663676416 | bytes 16777216 | tf_op jit(solution)/shard_map/grid/pallas_call | solution.py:543
  216.0 4.6 %all-to-all-start.1 = ((f32[8,64,8,128]{3,2,1,0:T(8,128)}), f32[8,64,8,128]{3,2,1,0:T(8,128)}, u32[]{:S(2)}, u32[]{:S(2)}) async-start(f32[8,64,8,128]{3,2,1,0:T(8,128)} %bitcast.34), calls=%async_computation.1 | async-start | bytes 4194304 | tf_op jit(solution)/shard_map/all_to_all | solution.py:732
  220.8 1.5 collective-permute-start.1
  222.3 1.4 collective-permute-start.2
  223.7 0.6 and_select_fusion.where_ref
  224.3 0.6 broadcast_multiply_fusion
  225.0 0.6 fusion.12
  225.6 103.9 %all-reduce.7.cloned.1.call-done = f32[32,64,128]{2,1,0:T(8,128)} async-done(((f32[32,64,128]{2,1,0:T(8,128)}), f32[32,64,128]{2,1,0:T(8,128)}) %all-reduce.7.cloned.1.call-update) | async-done | bytes 1048592 | tf_op jit(solution)/shard_map/psum | solution.py:836
  329.5 3.9 %fusion = f32[32,64,128]{2,1,0:T(8,128)} fusion(f32[32,64,128]{2,1,0:T(8,128)} %all-reduce.7.cloned.1.call-done, f32[32,64,64]{2,0,1:T(8,128)S(1)} %fusion.12), kind=kOutput, calls=%fused_computation.3 | convolution fusion | flops 201326592 | bytes 2621440 | tf_op jit(solution)/shard_map/akb,afk->baf/dot_general | solution.py:854
  333.4 2.6 copy.23.sphere_ref
  336.0 18.5 %muffin.1.muffin_ref = f32[128,4096]{1,0:T(8,128)} custom-call(s32[32]{0:T(128)} %types_ref.3, f32[4,64,4096]{2,1,0:T(8,128)} %get-tuple-element.31.table_ref, f32[32,4096]{1,0:T(8,128)} %get-tuple-element.32.phase_ref, f32[128,2048]{1,0:T(8,128)} %copy.23.sphere_ref, f32[1,4096]{1,0:T(1,128)} %bitcast.47, f32[4096,128]{1,0:T(8,128)} %refs_0_.1), custom_call_target="tpu_custom_call" | custom-call | flops 6442450944 | bytes 4194304 | tf_op jit(solution)/shard_map/muffin/pallas_call | solution.py:238
  354.5 15.6 %finish.1 = (f32[4096,128]{1,0:T(8,128)}, f32[4,128,128]{2,1,0:T(8,128)}) custom-call(s32[4096]{0:T(1024)} %convert_reduce_fusion.rank_ref, s32[4]{0:T(128)} %and_select_fusion.where_ref, f32[8,64,8,128]{3,2,1,0:T(8,128)} %all-to-all-done.1.back_ref, f32[128,4096]{1,0:T(8,128)} %muffin.1.muffin_ref, f32[4096,128]{1,0:T(8,128)} %refs_0_.1, ...), custom_call_target="tpu_custom_call" | custom-call | tf_op jit(solution)/shard_map/finish/pallas_call | solution.py:707
  370.1 12.6 %all_to_all.15 = f32[8,64,128]{2,1,0:T(8,128)S(1)} all-to-all(f32[8,64,128]{2,1,0:T(8,128)} %bitcast.37), channel_id=1, replica_groups=mesh['band'=4,'pw'=8] {'pw'}, dimensions={0} | all-to-all | bytes 524288 | tf_op jit(solution)/shard_map/all_to_all | solution.py:732
  382.7 0.6 reduce_sum.39
  (46 shorter events, 0.9 us)
Async XLA Ops:
  7.2 217.8 %copy-start = (f32[4,64,64]{2,1,0:T(8,128)S(1)}, f32[4,64,64]{2,1,0:T(8,128)}, u32[]{:S(2)}) copy-start(f32[4,64,64]{2,1,0:T(8,128)} %param.16) | copy-start | bytes 196612
  8.2 8.9 %copy-start.5 = (s32[4096]{0:T(1024)}, s32[4096]{0:T(1024)S(1)}, u32[]{:S(2)}) copy-start(s32[4096]{0:T(1024)S(1)} %multiply_add_fusion.1.key_ref) | copy-start | bytes 49156
  34.1 8.5 %copy-start.4 = (f32[8,64,64]{2,1,0:T(8,128)S(1)}, f32[8,64,64]{2,1,0:T(8,128)}, u32[]{:S(2)}) copy-start(f32[8,64,64]{2,1,0:T(8,128)} %param.17) | copy-start | bytes 393220
  34.1 11.4 %copy-start.6 = (f32[3,32]{1,0:T(4,128)S(1)}, f32[3,32]{1,0:T(4,128)}, u32[]{:S(2)}) copy-start(f32[3,32]{1,0:T(4,128)} %param.14) | copy-start | bytes 1156
  34.1 12.1 %copy-start.8 = (f32[4]{0:T(128)S(1)}, f32[4]{0:T(128)}, u32[]{:S(2)}) copy-start(f32[4]{0:T(128)} %param.15) | copy-start | bytes 52
  34.1 90.6 %all-to-all-start = ((f32[8,68,8,128]{3,2,1,0:T(8,128)}), f32[8,68,8,128]{3,2,1,0:T(8,128)S(1)}, u32[]{:S(2)}, u32[]{:S(2)}) async-start(f32[8,68,8,128]{3,2,1,0:T(8,128)} %broadcast_dynamic-update-slice_fusion), calls=%async_computation | async-start | bytes 4456448 | tf_op jit(solution)/shard_map/all_to_all | solution.py:732
  41.5 67.3 %all-gather.3.cloned.1.call-start = ((), (), s32[]{:S(2)}) async-start(), calls=%async_computation.4 | async-start | bytes 1511424 | tf_op jit(solution)/shard_map/all_gather | solution.py:802
  124.6 3.1 copy-start.2
  216.0 4.7 %copy-start.1 = (f32[4096,128]{1,0:T(8,128)S(1)}, f32[4096,128]{1,0:T(8,128)}, u32[]{:S(2)}) copy-start(f32[4096,128]{1,0:T(8,128)} %refs_0_.1) | copy-start | bytes 6291460
  216.0 8.3 %copy-start.3 = (s32[3,4096]{1,0:T(4,128)S(1)}, s32[3,4096]{1,0:T(4,128)}, u32[]{:S(2)}) copy-start(s32[3,4096]{1,0:T(4,128)} %miller_ref.1) | copy-start | bytes 147460
  216.0 8.9 %copy-start.7 = (s32[32]{0:T(128)S(1)}, s32[32]{0:T(128)}, u32[]{:S(2)}) copy-start(s32[32]{0:T(128)} %types_ref.3) | copy-start | bytes 388
  216.0 138.5 %all-to-all-start.1 = ((f32[8,64,8,128]{3,2,1,0:T(8,128)}), f32[8,64,8,128]{3,2,1,0:T(8,128)}, u32[]{:S(2)}, u32[]{:S(2)}) async-start(f32[8,64,8,128]{3,2,1,0:T(8,128)} %bitcast.34), calls=%async_computation.1 | async-start | bytes 4194304 | tf_op jit(solution)/shard_map/all_to_all | solution.py:732
  220.7 108.8 %all-reduce.7.cloned.1.call-start = ((), (), s32[]{:S(2)}) async-start(), calls=%async_computation.3 | async-start | bytes 2097152 | tf_op jit(solution)/shard_map/psum | solution.py:836
  220.7 133.8 %collective-permute-start = (f32[4096,128]{1,0:T(8,128)S(1)}, f32[4096,128]{1,0:T(8,128)}, u32[]{:S(2)}, u32[]{:S(2)}) collective-permute-start(f32[4096,128]{1,0:T(8,128)S(1)} %copy-done.1), channel_id=1, source_target_pairs={{0,8},{8,16},{16,24},{24,0},{1,9},{9,17},{17,25},{25,1},{2,10},{10... | collective-permute-start | bytes 6291464 | tf_op jit(solution)/shard_map/ppermute | solution.py:780
  220.8 133.7 %collective-permute-start.1 = (f32[4096,128]{1,0:T(8,128)S(1)}, f32[4096,128]{1,0:T(8,128)}, u32[]{:S(2)}, u32[]{:S(2)}) collective-permute-start(f32[4096,128]{1,0:T(8,128)S(1)} %copy-done.1), channel_id=1, source_target_pairs={{0,16},{8,24},{16,0},{24,8},{1,17},{9,25},{17,1},{25,9},{2,18},{10... | collective-permute-start | bytes 6291464 | tf_op jit(solution)/shard_map/ppermute | solution.py:780
  222.3 132.2 %collective-permute-start.2 = (f32[4096,128]{1,0:T(8,128)S(1)}, f32[4096,128]{1,0:T(8,128)}, u32[]{:S(2)}, u32[]{:S(2)}) collective-permute-start(f32[4096,128]{1,0:T(8,128)S(1)} %copy-done.1), channel_id=1, source_target_pairs={{0,24},{8,0},{16,8},{24,16},{1,25},{9,1},{17,9},{25,17},{2,26},{10... | collective-permute-start | bytes 6291464 | tf_op jit(solution)/shard_map/ppermute | solution.py:780
Sparse Core Ops, SparseCore 0:
  45.5 63.3 all-gather.2
  225.0 104.4 all-reduce.6

commit v4 on v3

--- a/solution.py
+++ b/solution.py
@@ -284,7 +284,7 @@
             send_ref[part, 2 * tile + 1] = jnp.concatenate([top[:, half:], low[:, half:]], axis=1)
         return carry
 
-    lax.fori_loop(0, waves // lanes, turn, 0)
+    lax.fori_loop(0, waves // lanes, turn, 0, unroll=4)
 
 
 def sort_call(rank, key, wave, parts, half):
@@ -437,7 +437,7 @@
         both = dot32(jnp.concatenate([high, low], axis=1), right)
         return both[:, :lanes] + both[:, lanes:]
 
-    many = 8
+    many = math.gcd(size, 16)
 
     chains = max(1, math.gcd(size // many, 4))
     groups = size // (many * chains)
@@ -500,7 +500,7 @@
         index = jnp.broadcast_to(slot_y_ref[pl.ds(block, 1), :], (pairs, lanes))
         return wanted, index
 
-    together = math.gcd(blocks, 8)
+    together = math.gcd(blocks, 16)
 
     def collect(group, carry):
         longest = 0
@@ -799,7 +799,8 @@
     pieces = [piece.reshape(-1, lanes) for piece in pieces]
     cuts = np.cumsum([piece.shape[0] for piece in pieces])
     pieces.append(jnp.zeros((-int(cuts[-1]) % 8, lanes), jnp.float32))
-    known = lax.all_gather(jnp.concatenate(pieces), "pw", axis=0, tiled=False)
+    known = jnp.concatenate(pieces)
+    known = exchange(jnp.broadcast_to(known[None], (pw_count,) + known.shape))
 
     send, sorted_key = sort_call(rank, key, wave_coeffs, pw_count, size)
     _, pairs = send.shape[1:3]

time: 391 us -> 356 us (0.910)
  Pallas kernels: 178 us -> 158 us
  waiting for transfers between devices: 137 us -> 118 us
    all_gather x1 -> x0, waiting for transfers between devices: 32.9 us -> none  [whole_step(): known = lax.all_gather(jnp.concatenate(pieces), 'pw', axis=0, tiled=False)]
    pallas_call x1, Pallas kernels: 88.3 us -> 72.1 us  [grid_call(): pl.pallas_call(functools.partial(grid_kernel, size=size, pitch=pitch, ban...]
    all_to_all x2 -> x3, waiting for transfers between devices: 0.01 us -> 14.5 us  [exchange(): return lax.all_to_all(array, 'pw', split_axis=0, concat_axis=0, tiled=True)]
    all_to_all x2 -> x3, starting transfers between devices: 12.1 us -> 15.6 us  [exchange(): return lax.all_to_all(array, 'pw', split_axis=0, concat_axis=0, tiled=True)]
  transfers between devices with their start and end apart: 7 -> 7, of which waited for: 2 -> 3; matrix products, arithmetic and copies ran while one was open for 5% -> 7% of each run, Pallas kernels for 15% -> 20%
where the time goes in v4:
time: 356 us
  Pallas kernels  158 us (44%)
  waiting for transfers between devices  118 us (33%)
  other arithmetic  19.8 us (6%)
  starting transfers between devices  18.6 us (5%)
  between operations  14.3 us (4%)
  blocking collectives  12.6 us (4%)
  local copies, waits for them, and re-layouts  9.77 us (3%)
  matrix products  4.56 us (1%)
    psum x1, waiting for transfers between devices, whole_step(): spheres = lax.psum(spheres, 'pw')  103 us
    pallas_call x1, Pallas kernels, grid_call(): pl.pallas_call(functools.partial(grid_kernel, size=size, pitch=pitch, ban...  72.1 us
    pallas_call x1, Pallas kernels, sphere_call(): pl.pallas_call(functools.partial(sphere_kernel, spacing=spacing), grid=(w...  26.6 us
    pallas_call x1, Pallas kernels, muffin_call(): pl.pallas_call(muffin_kernel, grid=(waves // block,), in_specs=[pl.BlockS...  18.6 us
    all_to_all x3, starting transfers between devices, exchange(): return lax.all_to_all(array, 'pw', split_axis=0, concat_axis=0, tiled=True)  15.6 us
    pallas_call x1, Pallas kernels, finish_call(): pl.pallas_call(finish_kernel, grid=(waves // block,), in_specs=[pl.BlockS...  15.6 us
    all_to_all x3, waiting for transfers between devices, exchange(): return lax.all_to_all(array, 'pw', split_axis=0, concat_axis=0, tiled=True)  14.5 us
    pallas_call x1, Pallas kernels, prepare_call(): pl.pallas_call(functools.partial(prepare_kernel, waves=waves, low_count=l...  13.4 us
  transfers between devices with their start and end apart: 7, of which 3 were waited for; matrix products, arithmetic and copies ran while one was open for 7% of the time, Pallas kernels for 20%

profile of v4, /device:TPU:0, one launch (start us, length us, event | category | flops | bytes accessed | tf_op | source)
XLA Modules:
  0.0 355.6 jit_solution(4786743489668418211)
XLA Ops:
  7.2 0.9 add_select_fusion.2
  8.2 1.0 convert_reduce_fusion.1
  9.2 1.1 copy.18
  10.3 0.1 reshape.138
  10.4 1.2 broadcast_in_dim.9
  11.6 7.3 %all-to-all-start = ((f32[8,328,128]{2,1,0:T(8,128)}), f32[8,328,128]{2,1,0:T(8,128)S(1)}, u32[]{:S(2)}, u32[]{:S(2)}) async-start(f32[8,328,128]{2,1,0:T(8,128)} %broadcast_in_dim.9), calls=%async_computation | async-start | bytes 2686976 | tf_op jit(solution)/shard_map/all_to_all | solution.py:732
  18.9 8.9 %convert_reduce_fusion.rank_ref = s32[4096]{0:T(1024)} fusion(s32[4096]{0:T(1024)S(1)} %bitcast.47, s32[4096]{0:T(1024)S(1)} %multiply_add_fusion.1.key_ref), kind=kLoop, calls=%fused_computation | loop fusion | flops 50327552 | bytes 49152 | tf_op jit(solution)/shard_map/reduce_sum | solution.py:786
  27.9 12.1 %sort.1 = (f32[8,68,8,128]{3,2,1,0:T(8,128)}, s32[4096]{0:T(1024)}) custom-call(s32[4096]{0:T(1024)} %convert_reduce_fusion.rank_ref, s32[4096]{0:T(1024)} %copy-done.5, f32[4096,128]{1,0:T(8,128)} %refs_0_.1), custom_call_target="tpu_custom_call" | custom-call | tf_op jit(solution)/shard_map/sort/pallas_call | solution.py:294
  40.0 0.7 convert_bitcast_fusion
  40.7 0.7 broadcast_dynamic-update-slice_fusion
  41.4 9.6 %all-to-all-done.known_ref = f32[8,328,128]{2,1,0:T(8,128)S(1)} async-done(((f32[8,328,128]{2,1,0:T(8,128)}), f32[8,328,128]{2,1,0:T(8,128)S(1)}, u32[]{:S(2)}, u32[]{:S(2)}) %all-to-all-start) | async-done | bytes 1343520 | tf_op jit(solution)/shard_map/all_to_all | solution.py:732
  51.0 1.1 copy-done.3
  52.1 3.6 %all-to-all-start.1 = ((f32[8,68,8,128]{3,2,1,0:T(8,128)}), f32[8,68,8,128]{3,2,1,0:T(8,128)S(1)}, u32[]{:S(2)}, u32[]{:S(2)}) async-start(f32[8,68,8,128]{3,2,1,0:T(8,128)} %broadcast_dynamic-update-slice_fusion), calls=%async_computation.1 | async-start | bytes 4456448 | tf_op jit(solution)/shard_map/all_to_all | solution.py:732
  55.9 0.7 copy.19
  56.6 0.7 copy.20.radii_ref
  57.4 0.1 add.158
  57.5 0.2 subtract_reduce-precision_fusion
  57.7 0.2 fusion.34
  57.8 0.2 fusion.38
  58.0 0.2 fusion.35
  58.2 0.7 pad_maximum_fusion.left_ref
  58.9 0.7 fusion.11.right_ref
  59.6 26.6 %sphere.1 = (f32[2048,128]{1,0:T(8,128)}, f32[4,64,4096]{2,1,0:T(8,128)}, f32[32,4096]{1,0:T(8,128)}) custom-call(s32[32]{0:T(128)} %types_ref.3, s32[3,4096]{1,0:T(4,128)} %miller_ref.1, f32[32,3]{1,0:T(8,128)} %bitcast.45, f32[4,1]{1,0:T(4,128)} %copy.20.radii_ref, f32[4096,128]{1,0:T(8,128)} %refs_0_.1), custom_call_target="tpu_custom_call" | custom-call | flops 6442450944 | bytes 4194304 | tf_op jit(solution)/shard_map/sphere/pallas_call | solution.py:180
  86.3 0.8 slice_convert_fusion.1
  87.1 0.6 fusion.33
  88.0 0.2 fusion.18
  88.2 13.4 %prepare.1 = (s32[8,512,128]{2,1,0:T(8,128)}, f32[8,512,128]{2,1,0:T(8,128)}) custom-call(f32[8,328,128]{2,1,0:T(8,128)} %copy-done.3, bf16[256,1024]{1,0:T(8,128)(2,1)} %constant.167.clone.lanes_ref, bf16[128,384]{1,0:T(8,128)(2,1)} %constant.168.clone.rows_ref), custom_call_target="tpu_custom_call" | custom-call | flops 2147483648 | bytes 131072 | tf_op jit(solution)/shard_map/prepare/pallas_call | solution.py:635
  101.5 0.5 compare_convert_fusion.deep_ref
  102.0 4.9 %all-to-all-done.1.compact_ref = f32[8,68,8,128]{3,2,1,0:T(8,128)S(1)} async-done(((f32[8,68,8,128]{3,2,1,0:T(8,128)}), f32[8,68,8,128]{3,2,1,0:T(8,128)S(1)}, u32[]{:S(2)}, u32[]{:S(2)}) %all-to-all-start.1) | async-done | bytes 2228256 | tf_op jit(solution)/shard_map/all_to_all | solution.py:732
  107.0 0.1 reshape.139
  107.1 0.3 add_select_fusion
  107.4 1.0 slice_reduce_fusion
  108.3 0.8 pad_add_fusion.slot_row_ref
  109.2 0.8 pad_add_fusion.1.slot_y_ref
  110.1 72.1 %grid.1 = f32[512,8,128]{2,1,0:T(8,128)} custom-call(s32[4096]{0:T(1024)} %get-tuple-element.38.window_ref, s32[64]{0:T(128)} %compare_convert_fusion.deep_ref, s32[512]{0:T(512)} %get-tuple-element.37.first_ref, s32[512]{0:T(512)} %get-tuple-element.36.last_ref, s32[4096,128]{1,0:T(8,128)} %bitcast.49, s32[512,128]{1,0:T(8,128)} %pad_add_fusion.slot_row_ref, ...), custom_call_target="tpu_custom_call" | custom-call | flops 9663676416 | bytes 16777216 | tf_op jit(solution)/shard_map/grid/pallas_call | solution.py:543
  182.2 4.6 %all-to-all-start.2 = ((f32[8,64,8,128]{3,2,1,0:T(8,128)}), f32[8,64,8,128]{3,2,1,0:T(8,128)}, u32[]{:S(2)}, u32[]{:S(2)}) async-start(f32[8,64,8,128]{3,2,1,0:T(8,128)} %bitcast.33), calls=%async_computation.2 | async-start | bytes 4194304 | tf_op jit(solution)/shard_map/all_to_all | solution.py:732
  186.9 1.6 collective-permute-start.1
  188.5 1.4 collective-permute-start.2
  189.9 0.6 and_select_fusion.where_ref
  190.5 0.6 broadcast_multiply_fusion
  191.1 0.6 fusion.12
  191.8 103.1 %all-reduce.7.cloned.1.call-done = f32[32,64,128]{2,1,0:T(8,128)} async-done(((f32[32,64,128]{2,1,0:T(8,128)}), f32[32,64,128]{2,1,0:T(8,128)}) %all-reduce.7.cloned.1.call-update) | async-done | bytes 1048592 | tf_op jit(solution)/shard_map/psum | solution.py:837
  294.9 3.9 %fusion = f32[32,64,128]{2,1,0:T(8,128)} fusion(f32[32,64,128]{2,1,0:T(8,128)} %all-reduce.7.cloned.1.call-done, f32[32,64,64]{2,0,1:T(8,128)S(1)} %fusion.12), kind=kOutput, calls=%fused_computation.3 | convolution fusion | flops 201326592 | bytes 2621440 | tf_op jit(solution)/shard_map/akb,afk->baf/dot_general | solution.py:855
  298.8 2.6 copy.23.sphere_ref
  301.4 18.6 %muffin.1.muffin_ref = f32[128,4096]{1,0:T(8,128)} custom-call(s32[32]{0:T(128)} %types_ref.3, f32[4,64,4096]{2,1,0:T(8,128)} %get-tuple-element.31.table_ref, f32[32,4096]{1,0:T(8,128)} %get-tuple-element.32.phase_ref, f32[128,2048]{1,0:T(8,128)} %copy.23.sphere_ref, f32[1,4096]{1,0:T(1,128)} %bitcast.46, f32[4096,128]{1,0:T(8,128)} %refs_0_.1), custom_call_target="tpu_custom_call" | custom-call | flops 6442450944 | bytes 4194304 | tf_op jit(solution)/shard_map/muffin/pallas_call | solution.py:238
  320.0 15.6 %finish.1 = (f32[4096,128]{1,0:T(8,128)}, f32[4,128,128]{2,1,0:T(8,128)}) custom-call(s32[4096]{0:T(1024)} %convert_reduce_fusion.rank_ref, s32[4]{0:T(128)} %and_select_fusion.where_ref, f32[8,64,8,128]{3,2,1,0:T(8,128)} %all-to-all-done.2.back_ref, f32[128,4096]{1,0:T(8,128)} %muffin.1.muffin_ref, f32[4096,128]{1,0:T(8,128)} %refs_0_.1, ...), custom_call_target="tpu_custom_call" | custom-call | tf_op jit(solution)/shard_map/finish/pallas_call | solution.py:707
  335.5 12.6 %all_to_all.20 = f32[8,64,128]{2,1,0:T(8,128)S(1)} all-to-all(f32[8,64,128]{2,1,0:T(8,128)} %bitcast.36), channel_id=1, replica_groups=mesh['band'=4,'pw'=8] {'pw'}, dimensions={0} | all-to-all | bytes 524288 | tf_op jit(solution)/shard_map/all_to_all | solution.py:732
  348.1 0.6 reduce_sum.39
  (46 shorter events, 1.1 us)
Async XLA Ops:
  7.2 184.0 %copy-start = (f32[4,64,64]{2,1,0:T(8,128)S(1)}, f32[4,64,64]{2,1,0:T(8,128)}, u32[]{:S(2)}) copy-start(f32[4,64,64]{2,1,0:T(8,128)} %param.16) | copy-start | bytes 196612
  11.6 39.4 %all-to-all-start = ((f32[8,328,128]{2,1,0:T(8,128)}), f32[8,328,128]{2,1,0:T(8,128)S(1)}, u32[]{:S(2)}, u32[]{:S(2)}) async-start(f32[8,328,128]{2,1,0:T(8,128)} %broadcast_in_dim.9), calls=%async_computation | async-start | bytes 2686976 | tf_op jit(solution)/shard_map/all_to_all | solution.py:732
  18.9 9.0 %copy-start.5 = (s32[4096]{0:T(1024)}, s32[4096]{0:T(1024)S(1)}, u32[]{:S(2)}) copy-start(s32[4096]{0:T(1024)S(1)} %multiply_add_fusion.1.key_ref) | copy-start | bytes 49156
  41.4 14.5 %copy-start.6 = (f32[3,32]{1,0:T(4,128)S(1)}, f32[3,32]{1,0:T(4,128)}, u32[]{:S(2)}) copy-start(f32[3,32]{1,0:T(4,128)} %param.14) | copy-start | bytes 1156
  41.4 15.2 %copy-start.8 = (f32[4]{0:T(128)S(1)}, f32[4]{0:T(128)}, u32[]{:S(2)}) copy-start(f32[4]{0:T(128)} %param.15) | copy-start | bytes 52
  51.0 1.1 copy-start.3
  52.1 54.9 %all-to-all-start.1 = ((f32[8,68,8,128]{3,2,1,0:T(8,128)}), f32[8,68,8,128]{3,2,1,0:T(8,128)S(1)}, u32[]{:S(2)}, u32[]{:S(2)}) async-start(f32[8,68,8,128]{3,2,1,0:T(8,128)} %broadcast_dynamic-update-slice_fusion), calls=%async_computation.1 | async-start | bytes 4456448 | tf_op jit(solution)/shard_map/all_to_all | solution.py:732
  107.0 3.1 copy-start.2
  182.1 4.7 %copy-start.1 = (f32[4096,128]{1,0:T(8,128)S(1)}, f32[4096,128]{1,0:T(8,128)}, u32[]{:S(2)}) copy-start(f32[4096,128]{1,0:T(8,128)} %refs_0_.1) | copy-start | bytes 6291460
  182.1 8.3 %copy-start.4 = (s32[3,4096]{1,0:T(4,128)S(1)}, s32[3,4096]{1,0:T(4,128)}, u32[]{:S(2)}) copy-start(s32[3,4096]{1,0:T(4,128)} %miller_ref.1) | copy-start | bytes 147460
  182.1 9.0 %copy-start.7 = (s32[32]{0:T(128)S(1)}, s32[32]{0:T(128)}, u32[]{:S(2)}) copy-start(s32[32]{0:T(128)} %types_ref.3) | copy-start | bytes 388
  182.2 137.8 %all-to-all-start.2 = ((f32[8,64,8,128]{3,2,1,0:T(8,128)}), f32[8,64,8,128]{3,2,1,0:T(8,128)}, u32[]{:S(2)}, u32[]{:S(2)}) async-start(f32[8,64,8,128]{3,2,1,0:T(8,128)} %bitcast.33), calls=%async_computation.2 | async-start | bytes 4194304 | tf_op jit(solution)/shard_map/all_to_all | solution.py:732
  186.8 108.1 %all-reduce.7.cloned.1.call-start = ((), (), s32[]{:S(2)}) async-start(), calls=%async_computation.4 | async-start | bytes 2097152 | tf_op jit(solution)/shard_map/psum | solution.py:837
  186.8 133.1 %collective-permute-start = (f32[4096,128]{1,0:T(8,128)S(1)}, f32[4096,128]{1,0:T(8,128)}, u32[]{:S(2)}, u32[]{:S(2)}) collective-permute-start(f32[4096,128]{1,0:T(8,128)S(1)} %copy-done.1), channel_id=1, source_target_pairs={{0,8},{8,16},{16,24},{24,0},{1,9},{9,17},{17,25},{25,1},{2,10},{10... | collective-permute-start | bytes 6291464 | tf_op jit(solution)/shard_map/ppermute | solution.py:780
  186.9 133.0 %collective-permute-start.1 = (f32[4096,128]{1,0:T(8,128)S(1)}, f32[4096,128]{1,0:T(8,128)}, u32[]{:S(2)}, u32[]{:S(2)}) collective-permute-start(f32[4096,128]{1,0:T(8,128)S(1)} %copy-done.1), channel_id=1, source_target_pairs={{0,16},{8,24},{16,0},{24,8},{1,17},{9,25},{17,1},{25,9},{2,18},{10... | collective-permute-start | bytes 6291464 | tf_op jit(solution)/shard_map/ppermute | solution.py:780
  188.5 131.5 %collective-permute-start.2 = (f32[4096,128]{1,0:T(8,128)S(1)}, f32[4096,128]{1,0:T(8,128)}, u32[]{:S(2)}, u32[]{:S(2)}) collective-permute-start(f32[4096,128]{1,0:T(8,128)S(1)} %copy-done.1), channel_id=1, source_target_pairs={{0,24},{8,0},{16,8},{24,16},{1,25},{9,1},{17,9},{25,17},{2,26},{10... | collective-permute-start | bytes 6291464 | tf_op jit(solution)/shard_map/ppermute | solution.py:780
Sparse Core Ops, SparseCore 0:
  191.1 103.7 all-reduce.6

commit v5 on v4

--- a/solution.py
+++ b/solution.py
@@ -79,13 +79,6 @@
     return columns
 
 
-def cas_matrix(grid_size):
-    across = jnp.arange(grid_size, dtype=jnp.int32)
-    phase = across[:, None] * across[None, :] % grid_size
-    angle = 2.0 * math.pi / grid_size * phase.astype(jnp.float32)
-    return (jnp.cos(angle) + jnp.sin(angle)) / math.sqrt(grid_size)
-
-
 def split_bf16(value):
     high = value.astype(jnp.bfloat16)
     low = (value - high.astype(jnp.float32)).astype(jnp.bfloat16)
@@ -563,7 +556,19 @@
     )(window, deep, first, last, code, slot_row, slot_y, field, left, right, compact)
 
 
-def prepare_kernel(known_ref, lanes_ref, rows_ref, code_ref, field_ref, *, waves, low_count, size):
+def prepare_kernel(
+    known_ref,
+    quarter_ref,
+    lanes_ref,
+    rows_ref,
+    code_ref,
+    field_ref,
+    *,
+    skip,
+    waves,
+    low_count,
+    size,
+):
     lanes = known_ref.shape[2]
     left_ids, right_ids = rows_ref.shape[0], lanes_ref.shape[0]
     field_rows = code_ref.shape[1] // 2
@@ -581,8 +586,8 @@
         )
 
     filled = lax.dot_general(
-        onehot(field_rows, left_ids),
-        onehot(field_rows + wave_rows, right_ids),
+        onehot(skip, left_ids),
+        onehot(skip + wave_rows, right_ids),
         (((1,), (1,)), ((), ())),
         preferred_element_type=jnp.float32,
     )
@@ -600,14 +605,15 @@
         for high in range(left_ids // size):
             first = (high * low_count + low) * size
             code_ref[0, first : first + size, :] = piece[high * size : (high + 1) * size, :]
-    field = known_ref[0, :field_rows, :]
+    field = quarter_ref[...].reshape(field_rows, lanes)
     for side in range(2):
         half = field[:, side * size : (side + 1) * size]
         field_ref[0, pl.ds(side, field_rows, stride=2), :] = jnp.concatenate([half, half], axis=1)
 
 
-def prepare_call(known, waves, planes_each, size):
+def prepare_call(known, quarters, waves, planes_each, size):
     parts, stored, lanes = known.shape
+    groups, _, skip, _ = quarters.shape
     low_count = math.gcd(planes_each, 4)
     high_count = planes_each // low_count
     lines = planes_each * size
@@ -633,10 +639,13 @@
         axis=1,
     )
     return pl.pallas_call(
-        functools.partial(prepare_kernel, waves=waves, low_count=low_count, size=size),
+        functools.partial(
+            prepare_kernel, skip=skip, waves=waves, low_count=low_count, size=size
+        ),
         grid=(parts,),
         in_specs=[
             pl.BlockSpec((1, stored, lanes), lambda i: (i, 0, 0)),
+            pl.BlockSpec((groups, 1, skip, lanes), lambda i: (0, i, 0, 0)),
             pl.BlockSpec(lanes_table.shape, lambda i: (0, 0)),
             pl.BlockSpec(rows_table.shape, lambda i: (0, 0)),
         ],
@@ -650,7 +659,7 @@
             flops=2 * parts * waves * lines * size, bytes_accessed=4 * parts * waves, transcendentals=0
         ),
         name="prepare",
-    )(known, jnp.asarray(lanes_table, jnp.bfloat16), jnp.asarray(rows_table, jnp.bfloat16))
+    )(known, quarters, jnp.asarray(lanes_table, jnp.bfloat16), jnp.asarray(rows_table, jnp.bfloat16))
 
 
 def finish_kernel(rank_ref, where_ref, back_ref, muffin_ref, *refs):
@@ -732,32 +741,22 @@
     return lax.all_to_all(array, "pw", split_axis=0, concat_axis=0, tiled=True)
 
 
-def round_high(value):
-    return lax.reduce_precision(value, 8, 7)
-
-
 def interstitial_tables(size):
-    table = cas_matrix(size)
-    high = round_high(table)
-    low = round_high(table - high)
-    zero = jnp.zeros_like(table)
-    left = jnp.concatenate(
-        [jnp.concatenate([high, high], axis=1), jnp.concatenate([low, zero], axis=1)], axis=0
-    )
-
-    def twice(block):
-        return jnp.concatenate(
-            [jnp.concatenate([block, zero], axis=1), jnp.concatenate([zero, block], axis=1)], axis=0
-        )
-
-    right = jnp.concatenate(
+    across = np.arange(size)
+    angle = 2.0 * np.pi / size * (across[:, None] * across[None, :] % size)
+    table = (np.cos(angle) + np.sin(angle)) / math.sqrt(size)
+    high = table.astype(jnp.bfloat16).astype(np.float64)
+    low = table - high
+    zero = np.zeros_like(table)
+    left = np.block([[high, high], [low, zero]])
+    both = np.eye(2)
+    right = np.block(
         [
-            jnp.concatenate([twice(high), twice(low)], axis=1),
-            jnp.concatenate([twice(high), jnp.zeros((2 * size, 2 * size))], axis=1),
-        ],
-        axis=0,
-    )
-    return left.astype(jnp.bfloat16), right.astype(jnp.bfloat16)
+            [np.kron(both, high), np.kron(both, low)],
+            [np.kron(both, high), np.kron(both, zero)],
+        ]
+    )
+    return jnp.asarray(left.astype(jnp.bfloat16)), jnp.asarray(right.astype(jnp.bfloat16))
 
 
 def whole_step(wave_coeffs, miller, atom_types, positions, sphere_radii, h_blocks, potential):
@@ -791,7 +790,9 @@
         (line[:, None] < jnp.arange(lines, dtype=jnp.int32)[None, :]).astype(jnp.int32), axis=0
     )
     pieces = [
-        jnp.transpose(potential, (0, 2, 1)),
+        lax.dynamic_index_in_dim(
+            jnp.transpose(potential, (0, 2, 1)).reshape(group_count, -1), group, 0
+        ),
         (plane // low_count * size + wrapped[0]).astype(jnp.float32),
         (plane % low_count * size + wrapped[1]).astype(jnp.float32),
         starts.astype(jnp.float32),
@@ -801,6 +802,7 @@
     pieces.append(jnp.zeros((-int(cuts[-1]) % 8, lanes), jnp.float32))
     known = jnp.concatenate(pieces)
     known = exchange(jnp.broadcast_to(known[None], (pw_count,) + known.shape))
+    quarters = lax.all_gather(known[:, : cuts[0]], "band", axis=0, tiled=False)
 
     send, sorted_key = sort_call(rank, key, wave_coeffs, pw_count, size)
     _, pairs = send.shape[1:3]
@@ -817,7 +819,7 @@
     )
     chosen = jnp.einsum("at,tfk->afk", onehot, h_blocks, precision=PRECISE)
 
-    codes, field = prepare_call(known, local_waves, planes_each, size)
+    codes, field = prepare_call(known, quarters, local_waves, planes_each, size)
     codes = codes.reshape(size * size, lanes)
     field = field.reshape(size * size, lanes)
     offsets = jnp.arange(pw_count, dtype=jnp.int32)[:, None]

time: 356 us -> 348 us (0.978)
  waiting for transfers between devices: 118 us -> 109 us
    all_to_all x3, waiting for transfers between devices: 14.5 us -> 6.04 us  [exchange(): return lax.all_to_all(array, 'pw', split_axis=0, concat_axis=0, tiled=True)]
  transfers between devices with their start and end apart: 7 -> 8, of which waited for: 3 -> 2; matrix products, arithmetic and copies ran while one was open for 7% -> 7% of each run, Pallas kernels for 20% -> 20%
where the time goes in v5:
time: 348 us; the launch traced here: 347 us
  Pallas kernels  158 us (45%)
  waiting for transfers between devices  109 us (31%)
  starting transfers between devices  21.3 us (6%)
  other arithmetic  16.9 us (5%)
  between operations  15.7 us (5%)
  blocking collectives  12.4 us (4%)
  local copies, waits for them, and re-layouts  9.22 us (3%)
  matrix products  4.56 us (1%)
    psum x1, waiting for transfers between devices, whole_step(): spheres = lax.psum(spheres, 'pw')  103 us
    pallas_call x1, Pallas kernels, grid_call(): pl.pallas_call(functools.partial(grid_kernel, size=size, pitch=pitch, ban...  71.9 us
    pallas_call x1, Pallas kernels, sphere_call(): pl.pallas_call(functools.partial(sphere_kernel, spacing=spacing), grid=(w...  26.7 us
    pallas_call x1, Pallas kernels, muffin_call(): pl.pallas_call(muffin_kernel, grid=(waves // block,), in_specs=[pl.BlockS...  18.6 us
    all_to_all x3, starting transfers between devices, exchange(): return lax.all_to_all(array, 'pw', split_axis=0, concat_axis=0, tiled=True)  18.1 us
    pallas_call x1, Pallas kernels, finish_call(): pl.pallas_call(finish_kernel, grid=(waves // block,), in_specs=[pl.BlockS...  15.6 us
    pallas_call x1, Pallas kernels, prepare_call(): pl.pallas_call(functools.partial(prepare_kernel, skip=skip, waves=waves,...  13.4 us
    all_to_all x1, blocking collectives, exchange(): return lax.all_to_all(array, 'pw', split_axis=0, concat_axis=0, tiled=True)  12.4 us
  transfers between devices with their start and end apart: 8, of which 2 were waited for; matrix products, arithmetic and copies ran while one was open for 7% of the time, Pallas kernels for 20%

profile of v5, /device:TPU:0, one launch (start us, length us, event | category | flops | bytes accessed | tf_op | source)
XLA Modules:
  0.0 347.1 jit_solution(1128391853458395127)
XLA Ops:
  8.0 0.9 add_select_fusion.2
  8.9 1.1 copy.26
  10.0 0.1 reshape.141
  10.2 1.0 convert_reduce_fusion.1
  11.3 0.8 broadcast_in_dim.9
  12.2 7.3 %all-to-all-start = ((f32[8,136,128]{2,1,0:T(8,128)}), f32[8,136,128]{2,1,0:T(8,128)S(1)}, u32[]{:S(2)}, u32[]{:S(2)}) async-start(f32[8,136,128]{2,1,0:T(8,128)} %broadcast_in_dim.9), calls=%async_computation | async-start | bytes 1114112 | tf_op jit(solution)/shard_map/all_to_all | solution.py:741
  19.5 8.9 %convert_reduce_fusion.rank_ref = s32[4096]{0:T(1024)} fusion(s32[4096]{0:T(1024)S(1)} %bitcast.50, s32[4096]{0:T(1024)S(1)} %multiply_add_fusion.1.key_ref), kind=kLoop, calls=%fused_computation | loop fusion | flops 50327552 | bytes 49152 | tf_op jit(solution)/shard_map/reduce_sum | solution.py:785
  28.5 12.1 %sort.1 = (f32[8,68,8,128]{3,2,1,0:T(8,128)}, s32[4096]{0:T(1024)}) custom-call(s32[4096]{0:T(1024)} %convert_reduce_fusion.rank_ref, s32[4096]{0:T(1024)} %copy-done.5, f32[4096,128]{1,0:T(8,128)} %refs_0_.1), custom_call_target="tpu_custom_call" | custom-call | tf_op jit(solution)/shard_map/sort/pallas_call | solution.py:287
  40.5 0.7 convert_bitcast_fusion
  41.2 0.7 broadcast_dynamic-update-slice_fusion
  41.9 6.1 %all-to-all-start.1 = ((f32[8,68,8,128]{3,2,1,0:T(8,128)}), f32[8,68,8,128]{3,2,1,0:T(8,128)S(1)}, u32[]{:S(2)}, u32[]{:S(2)}) async-start(f32[8,68,8,128]{3,2,1,0:T(8,128)} %broadcast_dynamic-update-slice_fusion), calls=%async_computation.1 | async-start | bytes 4456448 | tf_op jit(solution)/shard_map/all_to_all | solution.py:741
  48.1 0.2 all-gather.3.cloned.1.call-start
  48.3 0.1 broadcast_bitcast_fusion
  48.4 0.7 slice.74
  49.1 0.1 add.129
  49.2 0.1 add.130
  49.3 0.7 copy.27
  50.0 0.7 copy.28.radii_ref
  50.7 0.1 add.124
  50.8 26.7 %sphere.1 = (f32[2048,128]{1,0:T(8,128)}, f32[4,64,4096]{2,1,0:T(8,128)}, f32[32,4096]{1,0:T(8,128)}) custom-call(s32[32]{0:T(128)} %types_ref.3, s32[3,4096]{1,0:T(4,128)} %miller_ref.1, f32[32,3]{1,0:T(8,128)} %bitcast.48, f32[4,1]{1,0:T(4,128)} %copy.28.radii_ref, f32[4096,128]{1,0:T(8,128)} %refs_0_.1), custom_call_target="tpu_custom_call" | custom-call | flops 6442450944 | bytes 4194304 | tf_op jit(solution)/shard_map/sphere/pallas_call | solution.py:173
  77.5 0.1 convert_element_type.53
  77.6 0.6 fusion.18
  78.2 0.1 slice.70
  78.3 0.1 pad_add_fusion.2
  78.3 0.1 concatenate.18
  78.4 0.2 fusion.9
  78.6 0.5 compare_convert_fusion.deep_ref
  79.1 13.4 %prepare.1 = (s32[8,512,128]{2,1,0:T(8,128)}, f32[8,512,128]{2,1,0:T(8,128)}) custom-call(f32[8,136,128]{2,1,0:T(8,128)} %copy-done.3, f32[4,8,64,128]{3,2,1,0:T(8,128)} %bitcast.52, bf16[256,1024]{1,0:T(8,128)(2,1)} %constant.158.clone.lanes_ref, bf16[128,384]{1,0:T(8,128)(2,1)} %constant.159.clone.rows_ref), custom_call_target="tpu_custom_call" | custom-call | flops 2147483648 | bytes 131072 | tf_op jit(solution)/shard_map/prepare/pallas_call | solution.py:641
  92.5 6.0 %all-to-all-done.1.compact_ref = f32[8,68,8,128]{3,2,1,0:T(8,128)S(1)} async-done(((f32[8,68,8,128]{3,2,1,0:T(8,128)}), f32[8,68,8,128]{3,2,1,0:T(8,128)S(1)}, u32[]{:S(2)}, u32[]{:S(2)}) %all-to-all-start.1) | async-done | bytes 2228256 | tf_op jit(solution)/shard_map/all_to_all | solution.py:741
  98.6 0.1 reshape.143
  98.7 0.3 add_select_fusion
  99.0 1.0 slice_reduce_fusion
  100.0 0.8 pad_add_fusion.slot_row_ref
  100.9 0.9 pad_add_fusion.1.slot_y_ref
  101.7 71.9 %grid.1 = f32[512,8,128]{2,1,0:T(8,128)} custom-call(s32[4096]{0:T(1024)} %get-tuple-element.38.window_ref, s32[64]{0:T(128)} %compare_convert_fusion.deep_ref, s32[512]{0:T(512)} %get-tuple-element.37.first_ref, s32[512]{0:T(512)} %get-tuple-element.36.last_ref, s32[4096,128]{1,0:T(8,128)} %bitcast.53, s32[512,128]{1,0:T(8,128)} %pad_add_fusion.slot_row_ref, ...), custom_call_target="tpu_custom_call" | custom-call | flops 9663676416 | bytes 16777216 | tf_op jit(solution)/shard_map/grid/pallas_call | solution.py:536
  173.7 4.6 %all-to-all-start.2 = ((f32[8,64,8,128]{3,2,1,0:T(8,128)}), f32[8,64,8,128]{3,2,1,0:T(8,128)}, u32[]{:S(2)}, u32[]{:S(2)}) async-start(f32[8,64,8,128]{3,2,1,0:T(8,128)} %bitcast.35), calls=%async_computation.2 | async-start | bytes 4194304 | tf_op jit(solution)/shard_map/all_to_all | solution.py:741
  178.4 1.6 collective-permute-start.1
  180.0 1.4 collective-permute-start.2
  181.4 0.5 and_select_fusion.where_ref
  182.0 0.6 broadcast_multiply_fusion
  182.6 0.6 fusion.4
  183.2 102.8 %all-reduce.2.cloned.1.call-done = f32[32,64,128]{2,1,0:T(8,128)} async-done(((f32[32,64,128]{2,1,0:T(8,128)}), f32[32,64,128]{2,1,0:T(8,128)}) %all-reduce.2.cloned.1.call-update) | async-done | bytes 1048592 | tf_op jit(solution)/shard_map/psum | solution.py:839
  286.0 3.9 %fusion = f32[32,64,128]{2,1,0:T(8,128)} fusion(f32[32,64,128]{2,1,0:T(8,128)} %all-reduce.2.cloned.1.call-done, f32[32,64,64]{2,0,1:T(8,128)S(1)} %fusion.4), kind=kOutput, calls=%fused_computation.3 | convolution fusion | flops 201326592 | bytes 2621440 | tf_op jit(solution)/shard_map/akb,afk->baf/dot_general | solution.py:857
  289.9 2.6 copy.31.sphere_ref
  292.5 18.6 %muffin.1.muffin_ref = f32[128,4096]{1,0:T(8,128)} custom-call(s32[32]{0:T(128)} %types_ref.3, f32[4,64,4096]{2,1,0:T(8,128)} %get-tuple-element.31.table_ref, f32[32,4096]{1,0:T(8,128)} %get-tuple-element.32.phase_ref, f32[128,2048]{1,0:T(8,128)} %copy.31.sphere_ref, f32[1,4096]{1,0:T(1,128)} %bitcast.49, f32[4096,128]{1,0:T(8,128)} %refs_0_.1), custom_call_target="tpu_custom_call" | custom-call | flops 6442450944 | bytes 4194304 | tf_op jit(solution)/shard_map/muffin/pallas_call | solution.py:231
  311.1 15.6 %finish.1 = (f32[4096,128]{1,0:T(8,128)}, f32[4,128,128]{2,1,0:T(8,128)}) custom-call(s32[4096]{0:T(1024)} %convert_reduce_fusion.rank_ref, s32[4]{0:T(128)} %and_select_fusion.where_ref, f32[8,64,8,128]{3,2,1,0:T(8,128)} %all-to-all-done.2.back_ref, f32[128,4096]{1,0:T(8,128)} %muffin.1.muffin_ref, f32[4096,128]{1,0:T(8,128)} %refs_0_.1, ...), custom_call_target="tpu_custom_call" | custom-call | tf_op jit(solution)/shard_map/finish/pallas_call | solution.py:716
  326.6 12.4 %all_to_all.20 = f32[8,64,128]{2,1,0:T(8,128)S(1)} all-to-all(f32[8,64,128]{2,1,0:T(8,128)} %bitcast.38), channel_id=1, replica_groups=mesh['band'=4,'pw'=8] {'pw'}, dimensions={0} | all-to-all | bytes 524288 | tf_op jit(solution)/shard_map/all_to_all | solution.py:741
  339.0 0.6 reduce_sum.39
  (43 shorter events, 0.5 us)
Async XLA Ops:
  8.0 174.6 %copy-start = (f32[4,64,64]{2,1,0:T(8,128)S(1)}, f32[4,64,64]{2,1,0:T(8,128)}, u32[]{:S(2)}) copy-start(f32[4,64,64]{2,1,0:T(8,128)} %param.18) | copy-start | bytes 196612
  12.2 29.7 %all-to-all-start = ((f32[8,136,128]{2,1,0:T(8,128)}), f32[8,136,128]{2,1,0:T(8,128)S(1)}, u32[]{:S(2)}, u32[]{:S(2)}) async-start(f32[8,136,128]{2,1,0:T(8,128)} %broadcast_in_dim.9), calls=%async_computation | async-start | bytes 1114112 | tf_op jit(solution)/shard_map/all_to_all | solution.py:741
  19.5 9.0 %copy-start.5 = (s32[4096]{0:T(1024)}, s32[4096]{0:T(1024)S(1)}, u32[]{:S(2)}) copy-start(s32[4096]{0:T(1024)S(1)} %multiply_add_fusion.1.key_ref) | copy-start | bytes 49156
  41.9 7.4 %copy-start.6 = (f32[3,32]{1,0:T(4,128)S(1)}, f32[3,32]{1,0:T(4,128)}, u32[]{:S(2)}) copy-start(f32[3,32]{1,0:T(4,128)} %param.16) | copy-start | bytes 1156
  41.9 8.1 %copy-start.8 = (f32[4]{0:T(128)S(1)}, f32[4]{0:T(128)}, u32[]{:S(2)}) copy-start(f32[4]{0:T(128)} %param.17) | copy-start | bytes 52
  41.9 35.6 %copy-start.3 = (f32[8,136,128]{2,1,0:T(8,128)}, f32[8,136,128]{2,1,0:T(8,128)S(1)}, u32[]{:S(2)}) copy-start(f32[8,136,128]{2,1,0:T(8,128)S(1)} %all-to-all-done.known_ref) | copy-start | bytes 1671172
  41.9 56.6 %all-to-all-start.1 = ((f32[8,68,8,128]{3,2,1,0:T(8,128)}), f32[8,68,8,128]{3,2,1,0:T(8,128)S(1)}, u32[]{:S(2)}, u32[]{:S(2)}) async-start(f32[8,68,8,128]{3,2,1,0:T(8,128)} %broadcast_dynamic-update-slice_fusion), calls=%async_computation.1 | async-start | bytes 4456448 | tf_op jit(solution)/shard_map/all_to_all | solution.py:741
  48.1 31.1 %all-gather.3.cloned.1.call-start = ((), (), s32[]{:S(2)}) async-start(), calls=%async_computation.5 | async-start | bytes 1310720 | tf_op jit(solution)/shard_map/all_gather | solution.py:805
  98.6 3.2 copy-start.2
  173.7 4.7 %copy-start.1 = (f32[4096,128]{1,0:T(8,128)S(1)}, f32[4096,128]{1,0:T(8,128)}, u32[]{:S(2)}) copy-start(f32[4096,128]{1,0:T(8,128)} %refs_0_.1) | copy-start | bytes 6291460
  173.7 8.2 %copy-start.4 = (s32[3,4096]{1,0:T(4,128)S(1)}, s32[3,4096]{1,0:T(4,128)}, u32[]{:S(2)}) copy-start(s32[3,4096]{1,0:T(4,128)} %miller_ref.1) | copy-start | bytes 147460
  173.7 8.9 %copy-start.7 = (s32[32]{0:T(128)S(1)}, s32[32]{0:T(128)}, u32[]{:S(2)}) copy-start(s32[32]{0:T(128)} %types_ref.3) | copy-start | bytes 388
  173.7 137.4 %all-to-all-start.2 = ((f32[8,64,8,128]{3,2,1,0:T(8,128)}), f32[8,64,8,128]{3,2,1,0:T(8,128)}, u32[]{:S(2)}, u32[]{:S(2)}) async-start(f32[8,64,8,128]{3,2,1,0:T(8,128)} %bitcast.35), calls=%async_computation.2 | async-start | bytes 4194304 | tf_op jit(solution)/shard_map/all_to_all | solution.py:741
  178.3 107.7 %all-reduce.2.cloned.1.call-start = ((), (), s32[]{:S(2)}) async-start(), calls=%async_computation.4 | async-start | bytes 2097152 | tf_op jit(solution)/shard_map/psum | solution.py:839
  178.4 132.7 %collective-permute-start = (f32[4096,128]{1,0:T(8,128)S(1)}, f32[4096,128]{1,0:T(8,128)}, u32[]{:S(2)}, u32[]{:S(2)}) collective-permute-start(f32[4096,128]{1,0:T(8,128)S(1)} %copy-done.1), channel_id=1, source_target_pairs={{0,8},{8,16},{16,24},{24,0},{1,9},{9,17},{17,25},{25,1},{2,10},{10... | collective-permute-start | bytes 6291464 | tf_op jit(solution)/shard_map/ppermute | solution.py:779
  178.4 132.6 %collective-permute-start.1 = (f32[4096,128]{1,0:T(8,128)S(1)}, f32[4096,128]{1,0:T(8,128)}, u32[]{:S(2)}, u32[]{:S(2)}) collective-permute-start(f32[4096,128]{1,0:T(8,128)S(1)} %copy-done.1), channel_id=1, source_target_pairs={{0,16},{8,24},{16,0},{24,8},{1,17},{9,25},{17,1},{25,9},{2,18},{10... | collective-permute-start | bytes 6291464 | tf_op jit(solution)/shard_map/ppermute | solution.py:779
  180.0 131.1 %collective-permute-start.2 = (f32[4096,128]{1,0:T(8,128)S(1)}, f32[4096,128]{1,0:T(8,128)}, u32[]{:S(2)}, u32[]{:S(2)}) collective-permute-start(f32[4096,128]{1,0:T(8,128)S(1)} %copy-done.1), channel_id=1, source_target_pairs={{0,24},{8,0},{16,8},{24,16},{1,25},{9,1},{17,9},{25,17},{2,26},{10... | collective-permute-start | bytes 6291464 | tf_op jit(solution)/shard_map/ppermute | solution.py:779
Sparse Core Ops, SparseCore 0:
  51.0 18.0 all-gather.2
Sparse Core Ops, SparseCore 1:
  182.3 103.6 all-reduce.1
